TPU v7x, 16 devices: a whole 2x2x2 slice. The times are simulated.
16 devices in a mesh: dp: 4 (over z, y), tp: 4 (over x, core).
Axes of the slice: x: 2, y: 2, z: 2, core: 2. Of those that a mesh axis runs over, the one named last changes fastest.
Arguments:
- x: bfloat16 [16, 1024, 1152], P('dp', 'tp'), parts along dimension 0
- d_out: bfloat16 [16, 1024, 1152], P('dp', 'tp'), parts along dimension 0
- ln1_gain: float32 [1152], replicated
- ln1_bias: float32 [1152], replicated
- w_q: bfloat16 [1152, 16, 72], P(None, 'tp')
- b_q: bfloat16 [16, 72], P('tp')
- w_k: bfloat16 [1152, 16, 72], P(None, 'tp')
- w_v: bfloat16 [1152, 16, 72], P(None, 'tp')
- b_v: bfloat16 [16, 72], P('tp')
- w_o: bfloat16 [16, 72, 1152], P('tp')
- b_o: bfloat16 [1152], replicated
- ln2_gain: float32 [1152], replicated
- ln2_bias: float32 [1152], replicated
- w_1: bfloat16 [1152, 4304], P(None, 'tp')
- b_1: bfloat16 [4304], P('tp')
- w_2: bfloat16 [4304, 1152], P('tp')
- b_2: bfloat16 [1152], replicated
Outputs:
- output 1: bfloat16 [16, 1024, 1152], P('dp', 'tp'), parts along dimension 0
- output 2: bfloat16 [16, 1024, 1152], P('dp', 'tp'), parts along dimension 0
- output 3: float32 [4608], P('dp'), parts along dimension 0
- output 4: float32 [4608], P('dp'), parts along dimension 0
- output 5: bfloat16 [4608, 16, 72], P('dp', 'tp'), parts along dimension 0
- output 6: bfloat16 [64, 72], P(('dp', 'tp')), parts along dimension 0
- output 7: bfloat16 [4608, 16, 72], P('dp', 'tp'), parts along dimension 0
- output 8: bfloat16 [4608, 16, 72], P('dp', 'tp'), parts along dimension 0
- output 9: bfloat16 [64, 72], P(('dp', 'tp')), parts along dimension 0
- output 10: bfloat16 [64, 72, 1152], P(('dp', 'tp')), parts along dimension 0
- output 11: bfloat16 [4608], P('dp'), parts along dimension 0
- output 12: float32 [4608], P('dp'), parts along dimension 0
- output 13: float32 [4608], P('dp'), parts along dimension 0
- output 14: bfloat16 [4608, 4304], P('dp', 'tp'), parts along dimension 0
- output 15: bfloat16 [17216], P(('dp', 'tp')), parts along dimension 0
- output 16: bfloat16 [17216, 1152], P(('dp', 'tp')), parts along dimension 0
- output 17: bfloat16 [4608], P('dp'), parts along dimension 0
There are 4 independent parts. A program takes and returns all parts, laid end to end along the dimension named above; an argument that names none is the same for every part.
All inputs are finite; a program needn't handle non-finite values.
Results may differ from a plain program's by a relative error of at most 0.0181033.
Values are sent between devices in bfloat16 or wider.
A program may use at most 1 GiB of HBM per device.

v0:
```python
import math
import jax
import jax.numpy as jnp
from jax import lax
from jax.sharding import PartitionSpec as P

LN_EPS = 1e-6


def layer_norm(rows, ln_gain, ln_bias):
    row_mean = jnp.mean(rows, axis=-1, keepdims=True)
    centered = rows - row_mean
    variance = jnp.mean(centered * centered, axis=-1, keepdims=True)
    return centered * lax.rsqrt(variance + LN_EPS) * ln_gain + ln_bias


def gelu_tanh(pre_act):
    return jax.nn.gelu(pre_act, approximate=True)


def attention_core(queries, keys, values):
    att_scale = 1.0 / math.sqrt(queries.shape[-1])
    scores = jnp.einsum('bqhd,bkhd->bhqk', queries, keys, preferred_element_type=jnp.float32) * att_scale
    probs = jax.nn.softmax(scores, axis=-1).astype(jnp.bfloat16)
    mixed = jnp.einsum('bhqk,bkhd->bqhd', probs, values, preferred_element_type=jnp.float32)
    return mixed.astype(jnp.bfloat16)


def token_sum(grad_rows):
    return jnp.sum(grad_rows, axis=(0, 1), dtype=jnp.float32)


def solution(mesh):
    act_spec = P('dp', 'tp', None)
    replicated = P()
    head_w = P(None, 'tp', None)
    head_b = P('tp', None)
    grad_head_w = P('dp', 'tp', None)
    grad_head_b = P(('dp', 'tp'), None)
    grad_vec = P('dp')
    in_specs = (act_spec, act_spec, replicated, replicated, head_w, head_b, head_w, head_w, head_b,
                P('tp', None, None), replicated, replicated, replicated, P(None, 'tp'), P('tp'), P('tp', None), replicated)
    out_specs = (act_spec, act_spec, grad_vec, grad_vec, grad_head_w, grad_head_b, grad_head_w, grad_head_w, grad_head_b,
                 P(('dp', 'tp'), None, None), grad_vec, grad_vec, grad_vec, P('dp', 'tp'), P(('dp', 'tp')),
                 P(('dp', 'tp'), None), grad_vec)

    def gather_tokens(local_rows):
        return lax.all_gather(local_rows, 'tp', axis=1, tiled=True)

    def scatter_sum(part_sum):
        return lax.psum_scatter(part_sum, 'tp', scatter_dimension=1, tiled=True)

    def layer_step(x, d_out, ln1_gain, ln1_bias, w_q, b_q, w_k, w_v, b_v, w_o, b_o, ln2_gain, ln2_bias, w_1, b_1, w_2, b_2):
        x_f32 = x.astype(jnp.float32)
        h_one_f, ln1_pull = jax.vjp(layer_norm, x_f32, ln1_gain, ln1_bias)
        h_one = gather_tokens(h_one_f.astype(jnp.bfloat16))
        queries = (jnp.einsum('bnw,whd->bnhd', h_one, w_q, preferred_element_type=jnp.float32) + b_q).astype(jnp.bfloat16)
        keys = jnp.einsum('bnw,whd->bnhd', h_one, w_k, preferred_element_type=jnp.float32).astype(jnp.bfloat16)
        values = (jnp.einsum('bnw,whd->bnhd', h_one, w_v, preferred_element_type=jnp.float32) + b_v).astype(jnp.bfloat16)
        mixed, attn_pull = jax.vjp(attention_core, queries, keys, values)
        attn_out = scatter_sum(jnp.einsum('bnhd,hdw->bnw', mixed, w_o, preferred_element_type=jnp.float32))
        x_mid = (x_f32 + attn_out + b_o).astype(jnp.bfloat16)
        mid_f32 = x_mid.astype(jnp.float32)
        h_two_f, ln2_pull = jax.vjp(layer_norm, mid_f32, ln2_gain, ln2_bias)
        h_two = gather_tokens(h_two_f.astype(jnp.bfloat16))
        pre_act = (jnp.einsum('bnw,wf->bnf', h_two, w_1, preferred_element_type=jnp.float32) + b_1).astype(jnp.bfloat16)
        hidden_f, gelu_pull = jax.vjp(gelu_tanh, pre_act.astype(jnp.float32))
        hidden = hidden_f.astype(jnp.bfloat16)
        mlp_out = scatter_sum(jnp.einsum('bnf,fw->bnw', hidden, w_2, preferred_element_type=jnp.float32))
        y_out = (mid_f32 + mlp_out + b_2).astype(jnp.bfloat16)

        d_out_all = gather_tokens(d_out)
        d_hidden = jnp.einsum('bnw,fw->bnf', d_out_all, w_2, preferred_element_type=jnp.float32).astype(jnp.bfloat16)
        grad_w_2 = jnp.einsum('bnf,bnw->fw', hidden, d_out_all, preferred_element_type=jnp.float32).astype(jnp.bfloat16)
        (d_pre_f,) = gelu_pull(d_hidden.astype(jnp.float32))
        d_pre = d_pre_f.astype(jnp.bfloat16)
        grad_b_1 = token_sum(d_pre).astype(jnp.bfloat16)
        grad_w_1 = jnp.einsum('bnw,bnf->wf', h_two, d_pre, preferred_element_type=jnp.float32).astype(jnp.bfloat16)
        d_h_two = scatter_sum(jnp.einsum('bnf,wf->bnw', d_pre, w_1, preferred_element_type=jnp.float32)).astype(jnp.bfloat16)
        d_mid_ln, g_ln2_gain, g_ln2_bias = ln2_pull(d_h_two.astype(jnp.float32))
        d_mid = (d_out.astype(jnp.float32) + d_mid_ln).astype(jnp.bfloat16)
        d_mid_all = gather_tokens(d_mid)
        d_mixed = jnp.einsum('bnw,hdw->bnhd', d_mid_all, w_o, preferred_element_type=jnp.float32).astype(jnp.bfloat16)
        grad_w_o = jnp.einsum('bnhd,bnw->hdw', mixed, d_mid_all, preferred_element_type=jnp.float32).astype(jnp.bfloat16)
        d_query, d_key, d_value = attn_pull(d_mixed)
        grad_b_q = token_sum(d_query).astype(jnp.bfloat16)
        grad_b_v = token_sum(d_value).astype(jnp.bfloat16)
        grad_w_q = jnp.einsum('bnw,bnhd->whd', h_one, d_query, preferred_element_type=jnp.float32).astype(jnp.bfloat16)
        grad_w_k = jnp.einsum('bnw,bnhd->whd', h_one, d_key, preferred_element_type=jnp.float32).astype(jnp.bfloat16)
        grad_w_v = jnp.einsum('bnw,bnhd->whd', h_one, d_value, preferred_element_type=jnp.float32).astype(jnp.bfloat16)
        d_h_one_part = (jnp.einsum('bnhd,whd->bnw', d_query, w_q, preferred_element_type=jnp.float32)
                        + jnp.einsum('bnhd,whd->bnw', d_key, w_k, preferred_element_type=jnp.float32)
                        + jnp.einsum('bnhd,whd->bnw', d_value, w_v, preferred_element_type=jnp.float32))
        d_h_one = scatter_sum(d_h_one_part).astype(jnp.bfloat16)
        d_in_ln, g_ln1_gain, g_ln1_bias = ln1_pull(d_h_one.astype(jnp.float32))
        grad_x = (d_mid.astype(jnp.float32) + d_in_ln).astype(jnp.bfloat16)
        vec_sums = lax.psum(jnp.stack([g_ln1_gain, g_ln1_bias, token_sum(d_mid), g_ln2_gain, g_ln2_bias, token_sum(d_out)]), 'tp')
        return (y_out, grad_x, vec_sums[0], vec_sums[1], grad_w_q, grad_b_q, grad_w_k, grad_w_v, grad_b_v, grad_w_o,
                vec_sums[2].astype(jnp.bfloat16), vec_sums[3], vec_sums[4], grad_w_1, grad_b_1, grad_w_2,
                vec_sums[5].astype(jnp.bfloat16))

    return jax.shard_map(layer_step, mesh=mesh, in_specs=in_specs, out_specs=out_specs, check_vma=False)
```

profile of v0, /device:TPU:0, one launch (start us, length us, event | category | flops | bytes accessed | tf_op | source)
XLA Modules:
  0.0 1235.7 jit_solution(9661230726852905456)
XLA Ops:
  15.8 65.4 %all-gather.5.cloned.1.call-done = bf16[4,1024,1152]{2,1,0:T(8,128)(2,1)} async-done(((bf16[4,256,1152]{2,1,0:T(8,128)(2,1)}), bf16[4,1024,1152]{2,1,0:T(8,128)(2,1)}) %all-gather.5.cloned.1.call-update) | async-done | bytes 9437200 | tf_op jit(solution)/shard_map/all_gather | solution.py:48
  94.3 29.2 %fusion.161 = (f32[4,4,1024]{2,1,0:T(4,128)S(1)}, f32[4,4,1024,1024]{2,3,1,0:T(8,128)}) fusion(bf16[4,1024,4,72]{1,3,2,0:T(8,128)(2,1)} %add_convert_fusion, bf16[4,1024,4,72]{1,3,2,0:T(8,128)(2,1)} %fusion.118), kind=kOutput, calls=%fused_computation.169 | convolution fusion | flops 2466251776 | bytes 71892992 | tf_op jit(solution)/shard_map/jvp()/sub | solution.py:24
  123.6 32.8 %divide_convert_fusion = bf16[4,4,1024,1024]{2,3,1,0:T(8,128)(2,1)} fusion(f32[4,4,1024,1024]{2,3,1,0:T(8,128)} %get-tuple-element.40, f32[4,4,1024]{2,1,0:T(4,128)S(1)} %get-tuple-element.39), kind=kLoop, calls=%fused_computation.8 | loop fusion | flops 33554432 | bytes 100728832 | tf_op jit(solution)/shard_map/jvp()/convert_element_type | solution.py:24
  156.5 12.0 add_convert_fusion.1
  168.4 18.7 %convolution_convert_fusion.4 = bf16[4,4,72,1024]{3,2,1,0:T(8,128)(2,1)} fusion(bf16[4,1024,4,72]{1,3,2,0:T(8,128)(2,1)} %add_convert_fusion.1, bf16[4,4,1024,1024]{2,3,1,0:T(8,128)(2,1)} %divide_convert_fusion), kind=kOutput, calls=%fused_computation.142 | convolution fusion | flops 2417098752 | bytes 38273024 | tf_op jit(solution)/shard_map/jvp(bhqk,bkhd->bqhd)/dot_general | solution.py:25
  199.2 132.7 %reduce-scatter.5.cloned.1.call-done = f32[4,256,1152]{2,1,0:T(8,128)} async-done(((f32[4,1024,1152]{2,1,0:T(8,128)}), f32[4,256,1152]{2,1,0:T(8,128)}) %reduce-scatter.5.cloned.1.call-update) | async-done | bytes 4718608 | tf_op jit(solution)/shard_map/reduce_scatter | solution.py:51
  340.2 62.2 %all-gather.7.cloned.1.call-done = bf16[4,1024,1152]{2,1,0:T(8,128)(2,1)} async-done(((bf16[4,256,1152]{2,1,0:T(8,128)(2,1)}), bf16[4,1024,1152]{2,1,0:T(8,128)(2,1)}) %all-gather.7.cloned.1.call-update) | async-done | bytes 9437200 | tf_op jit(solution)/shard_map/all_gather | solution.py:48
  402.4 17.6 %fusion.23 = bf16[4,1024,1076]{1,2,0:T(8,128)(2,1)} fusion(bf16[4,1024,1152]{2,1,0:T(8,128)(2,1)} %all-gather.7.cloned.1.call-done, f32[1076]{0:T(1024)S(1)} %convert_element_type.173, bf16[1152,1076]{0,1:T(8,128)(2,1)} %param.30), kind=kOutput, calls=%fused_computation.36 | convolution fusion | flops 10163224576 | bytes 20735184 | tf_op jit(solution)/shard_map/bnw,wf->bnf/dot_general | solution.py:66
  420.1 46.5 %all-gather.9.cloned.1.call-done = bf16[4,1024,1152]{2,1,0:T(8,128)(2,1)} async-done(((bf16[4,256,1152]{2,1,0:T(8,128)(2,1)}), bf16[4,1024,1152]{2,1,0:T(8,128)(2,1)}) %all-gather.9.cloned.1.call-update) | async-done | bytes 9437200 | tf_op jit(solution)/shard_map/all_gather | solution.py:48
  466.6 27.5 %fusion.166 = (bf16[1076]{0:T(1024)(128)(2,1)}, bf16[4,1024,1076]{1,2,0:T(8,128)(2,1)}) fusion(bf16[4,1024,1076]{1,2,0:T(8,128)(2,1)} %fusion.23, bf16[4,1024,1152]{2,1,0:T(8,128)(2,1)} %all-gather.9.cloned.1.call-done, bf16[1076,1152]{1,0:T(8,128)(2,1)S(1)} %copy-done), kind=kOutput, calls=%fused_computation.170 | convolution fusion | flops 10260184064 | bytes 29547624 | tf_op jit(solution)/shard_map/bnw,fw->bnf/dot_general | solution.py:73
  494.0 20.4 %fusion.99 = f32[4,1024,1152]{2,1,0:T(8,128)} fusion(bf16[4,1024,1076]{1,2,0:T(8,128)(2,1)} %get-tuple-element.48, bf16[1152,1076]{0,1:T(8,128)(2,1)S(1)} %copy-done.42), kind=kOutput, calls=%fused_computation.119 | convolution fusion | flops 10154409984 | bytes 30168064 | tf_op jit(solution)/shard_map/bnf,wf->bnw/dot_general | solution.py:79
  514.5 23.1 %fusion.97 = f32[4,1024,1152]{2,1,0:T(8,128)} fusion(bf16[1076,1152]{1,0:T(8,128)(2,1)S(1)} %copy-done, bf16[4,1024,1076]{1,2,0:T(8,128)(2,1)} %fusion.23), kind=kOutput, calls=%fused_computation.117 | convolution fusion | flops 10198482944 | bytes 30168064 | tf_op jit(solution)/shard_map/bnf,fw->bnw/dot_general | solution.py:69
  538.3 109.5 %reduce-scatter.9.cloned.1.call-done = f32[4,256,1152]{2,1,0:T(8,128)} async-done(((f32[4,1024,1152]{2,1,0:T(8,128)}), f32[4,256,1152]{2,1,0:T(8,128)}) %reduce-scatter.9.cloned.1.call-update) | async-done | bytes 4718608 | tf_op jit(solution)/shard_map/reduce_scatter | solution.py:51
  656.8 126.7 %reduce-scatter.7.cloned.1.call-done = f32[4,256,1152]{2,1,0:T(8,128)} async-done(((f32[4,1024,1152]{2,1,0:T(8,128)}), f32[4,256,1152]{2,1,0:T(8,128)}) %reduce-scatter.7.cloned.1.call-update) | async-done | bytes 4718608 | tf_op jit(solution)/shard_map/reduce_scatter | solution.py:51
  791.0 62.8 %all-gather.11.cloned.1.call-done = bf16[4,1024,1152]{2,1,0:T(8,128)(2,1)} async-done(((bf16[4,256,1152]{2,1,0:T(8,128)(2,1)}), bf16[4,1024,1152]{2,1,0:T(8,128)(2,1)}) %all-gather.11.cloned.1.call-update) | async-done | bytes 9437200 | tf_op jit(solution)/shard_map/all_gather | solution.py:48
  864.6 17.5 %bitcast_reduce_fusion = (bf16[4,72]{1,0:T(4,128)(2,1)}, bf16[4,4,72,1024]{3,2,1,0:T(8,128)(2,1)}) fusion(bf16[4,4,1024,1024]{2,3,1,0:T(8,128)(2,1)} %divide_convert_fusion, bf16[4,1024,4,72]{1,3,2,0:T(8,128)(2,1)S(1)} %fusion.121), kind=kOutput, calls=%fused_computation.122 | convolution fusion | flops 2418278144 | bytes 38273600 | tf_op jit(solution)/shard_map/transpose(jvp(bhqk,bkhd->bqhd))/dot_general | solution.py:25
  882.0 33.8 %fusion.5 = (f32[4,4,1024]{2,1,0:T(4,128)S(1)}, bf16[4,4,1024,1024]{2,3,1,0:T(8,128)(2,1)}) fusion(f32[4,4,1024,1024]{2,3,1,0:T(8,128)} %get-tuple-element.40, f32[4,4,1024]{2,1,0:T(4,128)S(1)} %multiply_divide_fusion, bf16[4,1024,4,72]{1,3,2,0:T(8,128)(2,1)S(1)} %copy-done.8, bf16[4,1024,4,72]{1,3,2,0:T(8,128)(2,1)S(1)} %fusion.121), kind=kOutput, calls=%fused_computation.7 | convolution fusion | flops 2499788800 | bytes 105512960 | tf_op jit(solution)/shard_map/transpose(jvp(bhqk,bkhd->bqhd))/dot_general | solution.py:25
  915.8 41.3 %bitcast_reduce_fusion.1 = (bf16[4,72]{1,0:T(4,128)(2,1)}, bf16[4,4,1024,72]{2,3,1,0:T(8,128)(2,1)}) fusion(bf16[4,1024,4,72]{1,3,2,0:T(8,128)(2,1)} %fusion.118, bf16[4,4,1024,1024]{2,3,1,0:T(8,128)(2,1)} %get-tuple-element.42, f32[4,4,1024]{2,1,0:T(4,128)S(1)} %neg.13, f32[4,4,1024]{2,1,0:T(4,128)S(1)} %copy-done.16, ...), kind=kOutput, calls=%fused_computation.128 | convolution fusion | flops 4951654912 | bytes 40763968 | tf_op jit(solution)/shard_map/transpose(jvp(bqhd,bkhd->bhqk))/dot_general | solution.py:23
  957.2 45.5 %fusion.225 = f32[4,4,1024,1024]{2,3,1,0:T(8,128)} fusion(bf16[4,4,1024,1024]{2,3,1,0:T(8,128)(2,1)} %get-tuple-element.42, f32[4,4,1024]{2,1,0:T(4,128)S(1)} %neg.13, f32[4,4,1024]{2,1,0:T(4,128)S(1)} %copy-done.16, bf16[4,1024,4,72]{1,3,2,0:T(8,128)(2,1)S(1)} %copy-done.11, bf16[4,1024,4,72]{1,3,2,0:T(8,128)(2,1)} %fusion.118), kind=kOutput, calls=%fused_computation.5.clone.clone.1 | convolution fusion | flops 2533377024 | bytes 105512960 | tf_op jit(solution)/shard_map/jvp()/sub | solution.py:24
  1014.1 24.7 %convolution_convert_fusion.2 = bf16[4,4,1024,72]{2,3,1,0:T(8,128)(2,1)} fusion(bf16[4,1024,4,72]{1,3,2,0:T(8,128)(2,1)S(1)} %copy-done.11, f32[4,4,1024,1024]{2,3,1,0:T(8,128)} %fusion.225), kind=kOutput, calls=%fused_computation.140 | convolution fusion | flops 2417098752 | bytes 71827456 | tf_op jit(solution)/shard_map/transpose(jvp(bqhd,bkhd->bhqk))/dot_general | solution.py:23
  1049.8 22.1 %bitcast_add_fusion = f32[4,1024,1152]{2,1,0:T(8,128)} fusion(f32[4,1024,1152,1]{2,1,3,0:T(8,128)} %fusion.105, f32[4,1024,1152,1]{2,1,3,0:T(8,128)} %fusion.108, bf16[4,4,72,1024]{3,2,1,0:T(8,128)(2,1)S(1)} %copy-done.9, bf16[1152,4,72]{0,2,1:T(8,128)(2,1)S(1)} %copy-done.14), kind=kOutput, calls=%fused_computation.23 | convolution fusion | flops 2727346176 | bytes 59645952 | tf_op jit(solution)/shard_map/bnhd,whd->bnw/dot_general | solution.py:93
  1071.9 19.8 %fusion.40 = bf16[1152,1076]{0,1:T(8,128)(2,1)} fusion(bf16[4,1024,1152]{2,1,0:T(8,128)(2,1)} %all-gather.7.cloned.1.call-done, bf16[4,1024,1076]{1,2,0:T(8,128)(2,1)} %get-tuple-element.48), kind=kOutput, calls=%fused_computation.56 | convolution fusion | flops 10155649024 | bytes 20730880 | tf_op jit(solution)/shard_map/bnw,bnf->wf/dot_general | solution.py:78
  1091.8 19.0 %fusion.41 = bf16[1076,1152]{1,0:T(8,128)(2,1)} fusion(bf16[4,1024,1152]{2,1,0:T(8,128)(2,1)S(1)} %bitcast.213, bf16[4,1024,1076]{1,2,0:T(8,128)(2,1)} %fusion.23), kind=kOutput, calls=%fused_computation.57 | convolution fusion | flops 10199721984 | bytes 20730880 | tf_op jit(solution)/shard_map/bnf,bnw->fw/dot_general | solution.py:74
  1133.8 71.4 %reduce-scatter.11.cloned.1.call-done = f32[4,256,1152]{2,1,0:T(8,128)} async-done(((f32[4,1024,1152]{2,1,0:T(8,128)}), f32[4,256,1152]{2,1,0:T(8,128)}) %reduce-scatter.11.cloned.1.call-update) | async-done | bytes 4718608 | tf_op jit(solution)/shard_map/reduce_scatter | solution.py:51
  (172 shorter events, 138.5 us)
Async XLA Ops:
  7.2 459.4 %copy-start = (bf16[1076,1152]{1,0:T(8,128)(2,1)S(1)}, bf16[1076,1152]{1,0:T(8,128)(2,1)}, u32[]{:S(2)}) copy-start(bf16[1076,1152]{1,0:T(8,128)(2,1)} %param.32) | copy-start | bytes 7437316
  7.2 74.0 %all-gather.5.cloned.1.call-start = ((), (), s32[]{:S(2)}) async-start(), calls=%async_computation.4 | async-start | bytes 11796480 | tf_op jit(solution)/shard_map/all_gather | solution.py:48
  15.5 316.4 %reduce-scatter.5.cloned.1.call-start = ((), (), s32[]{:S(2)}) async-start(), calls=%async_computation.5 | async-start | bytes 23592960 | tf_op jit(solution)/shard_map/reduce_scatter | solution.py:51
  15.8 74.0 %copy-start.44 = (bf16[1152,4,72]{0,2,1:T(8,128)(2,1)S(1)}, bf16[1152,4,72]{0,2,1:T(8,128)(2,1)}, u32[]{:S(2)}) copy-start(bf16[1152,4,72]{0,2,1:T(8,128)(2,1)} %param.21) | copy-start | bytes 1990660
  123.6 32.9 %copy-start.15 = (f32[4,4,1024]{2,1,0:T(4,128)}, f32[4,4,1024]{2,1,0:T(4,128)S(1)}, u32[]{:S(2)}) copy-start(f32[4,4,1024]{2,1,0:T(4,128)S(1)} %get-tuple-element.39) | copy-start | bytes 196612
  123.6 32.9 %copy-start.13 = (bf16[1152,4,72]{0,2,1:T(8,128)(2,1)S(1)}, bf16[1152,4,72]{0,2,1:T(8,128)(2,1)}, u32[]{:S(2)}) copy-start(bf16[1152,4,72]{0,2,1:T(8,128)(2,1)} %param.24) | copy-start | bytes 1990660
  198.6 203.9 %all-gather.7.cloned.1.call-start = ((), (), s32[]{:S(2)}) async-start(), calls=%async_computation.6 | async-start | bytes 11796480 | tf_op jit(solution)/shard_map/all_gather | solution.py:48
  199.2 138.0 %copy-start.19 = (f32[1152]{0:T(1024)S(1)}, f32[1152]{0:T(1024)}, u32[]{:S(2)}) copy-start(f32[1152]{0:T(1024)} %param.28) | copy-start | bytes 13828
  199.2 138.0 %copy-start.35 = (f32[1152]{0:T(1024)S(1)}, f32[1152]{0:T(1024)}, u32[]{:S(2)}) copy-start(f32[1152]{0:T(1024)} %param.29) | copy-start | bytes 13828
  339.6 127.0 %all-gather.9.cloned.1.call-start = ((), (), s32[]{:S(2)}) async-start(), calls=%async_computation.8 | async-start | bytes 11796480 | tf_op jit(solution)/shard_map/all_gather | solution.py:48
  340.2 307.7 %reduce-scatter.9.cloned.1.call-start = ((), (), s32[]{:S(2)}) async-start(), calls=%async_computation.9 | async-start | bytes 23592960 | tf_op jit(solution)/shard_map/reduce_scatter | solution.py:51
  514.5 269.1 %reduce-scatter.7.cloned.1.call-start = ((), (), s32[]{:S(2)}) async-start(), calls=%async_computation.7 | async-start | bytes 23592960 | tf_op jit(solution)/shard_map/reduce_scatter | solution.py:51
  537.6 110.2 %copy-start.5 = (bf16[4,256,1152]{2,1,0:T(8,128)(2,1)S(1)}, bf16[4,256,1152]{2,1,0:T(8,128)(2,1)}, u32[]{:S(2)}) copy-start(bf16[4,256,1152]{2,1,0:T(8,128)(2,1)} %copy-done.4) | copy-start | bytes 7077892
  537.7 316.1 %all-gather.11.cloned.1.call-start = ((), (), s32[]{:S(2)}) async-start(), calls=%async_computation.10 | async-start | bytes 11796480 | tf_op jit(solution)/shard_map/all_gather | solution.py:48
  656.8 134.2 %copy-start.16 = (f32[4,4,1024]{2,1,0:T(4,128)S(1)}, f32[4,4,1024]{2,1,0:T(4,128)}, u32[]{:S(2)}) copy-start(f32[4,4,1024]{2,1,0:T(4,128)} %copy-done.15) | copy-start | bytes 196612
  791.0 414.3 %reduce-scatter.11.cloned.1.call-start = ((), (), s32[]{:S(2)}) async-start(), calls=%async_computation.11 | async-start | bytes 23592960 | tf_op jit(solution)/shard_map/reduce_scatter | solution.py:51
  915.8 41.4 %copy-start.11 = (bf16[4,1024,4,72]{1,3,2,0:T(8,128)(2,1)S(1)}, bf16[4,1024,4,72]{1,3,2,0:T(8,128)(2,1)}, u32[]{:S(2)}) copy-start(bf16[4,1024,4,72]{1,3,2,0:T(8,128)(2,1)} %add_convert_fusion) | copy-start | bytes 7077892
  957.2 45.5 %copy-start.45 = (bf16[1152,4,72]{0,2,1:T(8,128)(2,1)S(1)}, bf16[1152,4,72]{0,2,1:T(8,128)(2,1)}, u32[]{:S(2)}) copy-start(bf16[1152,4,72]{0,2,1:T(8,128)(2,1)} %param.21) | copy-start | bytes 1990660
  1071.9 49.1 %slice-start = ((s8[9437184]{0:T(1024)(128)(4,1)}), s8[1048576]{0:T(1024)(128)(4,1)S(1)}, s32[]{:S(2)}) async-start(s8[9437184]{0:T(1024)(128)(4,1)} %bitcast.210), calls=%async_computation.12 | async-start | bytes 2097152
  1129.4 75.8 %copy-start.3 = (bf16[4,256,1152]{2,1,0:T(8,128)(2,1)S(1)}, bf16[4,256,1152]{2,1,0:T(8,128)(2,1)}, u32[]{:S(2)}) copy-start(bf16[4,256,1152]{2,1,0:T(8,128)(2,1)} %param.17) | copy-start | bytes 7077892
  1129.4 75.8 %copy-start.18 = (f32[4,256]{1,0:T(4,128)S(1)}, f32[4,256]{1,0:T(4,128)}, u32[]{:S(2)}) copy-start(f32[4,256]{1,0:T(4,128)} %copy-done.17) | copy-start | bytes 12292
  1129.4 75.8 %copy-start.21 = (f32[1152]{0:T(1024)S(1)}, f32[1152]{0:T(1024)}, u32[]{:S(2)}) copy-start(f32[1152]{0:T(1024)} %param.19) | copy-start | bytes 13828
  1133.8 75.0 %copy-start.25 = (f32[4,256]{1,0:T(4,128)S(1)}, f32[4,256]{1,0:T(4,128)}, u32[]{:S(2)}) copy-start(f32[4,256]{1,0:T(4,128)} %copy-done.24) | copy-start | bytes 12292
  1133.8 75.1 %copy-start.23 = (f32[4,256]{1,0:T(4,128)S(1)}, f32[4,256]{1,0:T(4,128)}, u32[]{:S(2)}) copy-start(f32[4,256]{1,0:T(4,128)} %copy-done.22) | copy-start | bytes 12292
  (37 other events, 383.1 us)
Sparse Core Ops, SparseCore 0:
  15.7 65.5 all-gather.4
  198.7 133.2 reduce-scatter.4
  339.7 62.6 all-gather.6
  403.8 62.6 all-gather.8
  514.6 133.2 reduce-scatter.8
  650.3 133.2 reduce-scatter.6
  791.1 62.6 all-gather.10
  1072.0 133.2 reduce-scatter.10
where the time goes:
time: 1240 us
  waiting for transfers between devices  678 us (55%)
  matrix products  450 us (36%)
  other arithmetic  73.2 us (6%)
  between operations  14.9 us (1%)
    reduce_scatter x4, waiting for transfers between devices, scatter_sum(): return lax.psum_scatter(part_sum, 'tp', scatter_dimension=1, tiled=True)  440 us
    all_gather x4, waiting for transfers between devices, gather_tokens(): return lax.all_gather(local_rows, 'tp', axis=1, tiled=True)  237 us
    sub x2, matrix products, attention_core(): probs = jax.nn.softmax(scores, axis=-1).astype(jnp.bfloat16)  74.8 us
    dot_general x3, matrix products, attention_core(): jnp.einsum('bhqk,bkhd->bqhd', probs, values, preferred_element_type=jnp.f...  69.9 us
    dot_general x2, matrix products, attention_core(): jnp.einsum('bqhd,bkhd->bhqk', queries, keys, preferred_element_type=jnp.f...  66.1 us
    convert_element_type x1, other arithmetic, attention_core(): probs = jax.nn.softmax(scores, axis=-1).astype(jnp.bfloat16)  32.8 us
    dot_general x1, matrix products, layer_step(): jnp.einsum('bnw,fw->bnf', d_out_all, w_2, preferred_element_type=jnp.floa...  27.5 us
  transfers between devices with their start and end apart: 8, of which 8 were waited for; matrix products, arithmetic and copies ran while one was open for 9% of the time, Pallas kernels for 0%

commit v1 on v0

v1 whole, which is shorter than its diff:
```python
import math
import jax
import jax.numpy as jnp
from jax import lax
from jax.experimental import pallas as pl
from jax.experimental.pallas import tpu as pltpu
from jax.sharding import PartitionSpec as P

LN_EPS = 1e-6
HEAD = 72
PAIR = 2 * HEAD
QBLK = 256
F32 = jnp.float32
BF16 = jnp.bfloat16
LOG2E = 1.4426950408889634


def layer_norm(rows, ln_gain, ln_bias):
    row_mean = jnp.mean(rows, axis=-1, keepdims=True)
    centered = rows - row_mean
    variance = jnp.mean(centered * centered, axis=-1, keepdims=True)
    return centered * lax.rsqrt(variance + LN_EPS) * ln_gain + ln_bias


def gelu_tanh(pre_act):
    return jax.nn.gelu(pre_act, approximate=True)


def dot(a, b):
    return jnp.dot(a, b, preferred_element_type=F32)


def dot_nt(a, b):
    return lax.dot_general(a, b, (((1,), (1,)), ((), ())), preferred_element_type=F32)


def dot_tn(a, b):
    return lax.dot_general(a, b, (((0,), (0,)), ((), ())), preferred_element_type=F32)


def attn_fwd_kernel(q_ref, k_ref, v_ref, o_ref, l_ref):
    tokens = q_ref.shape[1]
    coef = LOG2E / math.sqrt(HEAD)
    q_all = q_ref[...].astype(F32)
    k_all = k_ref[...].astype(F32)
    v_all = v_ref[...].astype(F32)
    keys = [k_all[h * HEAD:(h + 1) * HEAD].T.astype(BF16) for h in range(2)]
    vals = [v_all[h * HEAD:(h + 1) * HEAD].astype(BF16) for h in range(2)]
    quer = [q_all[h * HEAD:(h + 1) * HEAD].astype(BF16) for h in range(2)]
    for start in range(0, tokens, QBLK):
        outs = []
        for h in range(2):
            s = dot(keys[h], quer[h][:, start:start + QBLK])
            top = jnp.max(s, axis=0, keepdims=True)
            e = jnp.exp2((s - top) * coef)
            total = jnp.sum(e, axis=0, keepdims=True)
            p = (e * (1.0 / total)).astype(BF16)
            outs.append(dot(vals[h], p))
            l_ref[0, h:h + 1, start:start + QBLK] = top * coef + jnp.log2(total)
        o_ref[:, start:start + QBLK] = jnp.concatenate(outs, axis=0).astype(BF16)


def attn_bwd_kernel(q_ref, k_ref, v_ref, g_ref, l_ref, d_ref, dk_acc, dv_acc):
    tokens = q_ref.shape[1]
    scale = 1.0 / math.sqrt(HEAD)
    coef = LOG2E * scale
    q_all = q_ref[...].astype(F32)
    k_all = k_ref[...].astype(F32)
    v_all = v_ref[...].astype(F32)
    g_all = g_ref[...].astype(F32)

    def head(a, h):
        return a[h * HEAD:(h + 1) * HEAD]

    k_t = [head(k_all, h).astype(BF16) for h in range(2)]
    keys = [head(k_all, h).T.astype(BF16) for h in range(2)]
    vals = [head(v_all, h).T.astype(BF16) for h in range(2)]
    q_t = [head(q_all, h).astype(BF16) for h in range(2)]
    q_n = [head(q_all, h).T.astype(BF16) for h in range(2)]
    g_t = [head(g_all, h).astype(BF16) for h in range(2)]
    g_n = [head(g_all, h).T.astype(BF16) for h in range(2)]
    for start in range(0, tokens, QBLK):
        cols = slice(start, start + QBLK)
        dqs = []
        for h in range(2):
            s = dot(keys[h], q_t[h][:, cols])
            p = jnp.exp2(s * coef - l_ref[0, h:h + 1, cols])
            dp = dot(vals[h], g_t[h][:, cols]).astype(BF16).astype(F32)
            delta = jnp.sum(p * dp, axis=0, keepdims=True)
            ds = (p * ((dp - delta) * scale)).astype(BF16)
            dv = dot(p.astype(BF16), g_n[h][cols])
            dk = dot(ds, q_n[h][cols])
            if start == 0:
                dv_acc[h] = dv
                dk_acc[h] = dk
            else:
                dv_acc[h] += dv
                dk_acc[h] += dk
            dqs.append(dot(k_t[h], ds))
        d_ref[0, :, cols] = jnp.concatenate(dqs, axis=0).astype(BF16)
    d_ref[1] = jnp.concatenate([dk_acc[h].T for h in range(2)], axis=0).astype(BF16)
    d_ref[2] = jnp.concatenate([dv_acc[h].T for h in range(2)], axis=0).astype(BF16)


def attn_fwd(qkv):
    rows, tokens = qkv.shape
    heads_rows = rows // 3
    pairs = heads_rows // PAIR
    spec = lambda off: pl.BlockSpec((PAIR, tokens), lambda i: (off * pairs + i, 0))
    flops = 4 * heads_rows * tokens * tokens
    return pl.pallas_call(
        attn_fwd_kernel,
        grid=(pairs,),
        in_specs=[spec(0), spec(1), spec(2)],
        out_specs=[spec(0), pl.BlockSpec((1, 8, tokens), lambda i: (i, 0, 0))],
        out_shape=[jax.ShapeDtypeStruct((heads_rows, tokens), BF16), jax.ShapeDtypeStruct((pairs, 8, tokens), F32)],
        cost_estimate=pl.CostEstimate(flops=flops * 4, bytes_accessed=8 * heads_rows * tokens, transcendentals=0),
        name="attn_fwd",
    )(qkv, qkv, qkv)


def attn_bwd(qkv, d_mixed, lse):
    rows, tokens = qkv.shape
    heads_rows = rows // 3
    pairs = heads_rows // PAIR
    spec = lambda off: pl.BlockSpec((PAIR, tokens), lambda i: (off * pairs + i, 0))
    flops = 10 * heads_rows * tokens * tokens
    grads = pl.pallas_call(
        attn_bwd_kernel,
        grid=(pairs,),
        in_specs=[spec(0), spec(1), spec(2), spec(0), pl.BlockSpec((1, 8, tokens), lambda i: (i, 0, 0))],
        out_specs=pl.BlockSpec((3, PAIR, tokens), lambda i: (0, i, 0)),
        out_shape=jax.ShapeDtypeStruct((3, heads_rows, tokens), BF16),
        scratch_shapes=[pltpu.VMEM((2, tokens, HEAD), F32), pltpu.VMEM((2, tokens, HEAD), F32)],
        cost_estimate=pl.CostEstimate(flops=flops * 4, bytes_accessed=16 * heads_rows * tokens, transcendentals=0),
        name="attn_bwd",
    )(qkv, qkv, qkv, d_mixed, lse)
    return grads.reshape(rows, tokens)


def solution(mesh):
    act_spec = P('dp', 'tp', None)
    replicated = P()
    head_w = P(None, 'tp', None)
    head_b = P('tp', None)
    grad_head_w = P('dp', 'tp', None)
    grad_head_b = P(('dp', 'tp'), None)
    grad_vec = P('dp')
    in_specs = (act_spec, act_spec, replicated, replicated, head_w, head_b, head_w, head_w, head_b,
                P('tp', None, None), replicated, replicated, replicated, P(None, 'tp'), P('tp'), P('tp', None), replicated)
    out_specs = (act_spec, act_spec, grad_vec, grad_vec, grad_head_w, grad_head_b, grad_head_w, grad_head_w, grad_head_b,
                 P(('dp', 'tp'), None, None), grad_vec, grad_vec, grad_vec, P('dp', 'tp'), P(('dp', 'tp')),
                 P(('dp', 'tp'), None), grad_vec)

    def swap(value, k):
        return lax.ppermute(value, 'tp', [(i, i ^ k) for i in range(4)])

    def send(block):
        return block, swap(block, 1), swap(block, 2)

    def land(sent, dep):
        own, near, two = sent
        two, _ = lax.optimization_barrier((two, dep))
        return [own, near, two, swap(two, 1)]

    def layer_step(x, d_out, ln1_gain, ln1_bias, w_q, b_q, w_k, w_v, b_v, w_o, b_o, ln2_gain, ln2_bias, w_1, b_1, w_2, b_2):
        me = lax.axis_index('tp')
        width = x.shape[2]
        slab = x.shape[1]
        local_rows = w_o.shape[0] * w_o.shape[1]

        def image(shard, k):
            return lax.dynamic_index_in_dim(shard, me ^ k, 0, keepdims=False)

        def to_image(shard):
            return jnp.concatenate([image(shard, 0)] + [swap(image(shard, k), k) for k in (1, 2, 3)], axis=0)

        def to_tokens(rows):
            parts = [rows[:slab]] + [swap(rows[k * slab:(k + 1) * slab], k) for k in (1, 2, 3)]
            stacked = jnp.stack(parts)
            return jnp.stack([lax.dynamic_index_in_dim(stacked, me ^ i, 0, keepdims=False) for i in range(4)])

        x_img = to_image(x)
        w_qkv_own = jnp.concatenate([w.reshape(width, local_rows).T for w in (w_q, w_k, w_v)], axis=0)
        w_qkv_sent = send(w_qkv_own)
        w_out_sent = send(w_o.reshape(local_rows, width))
        bias_own = jnp.concatenate([b_q.reshape(-1).astype(F32), b_v.reshape(-1).astype(F32), b_1.astype(F32)])
        biases = send(bias_own)
        biases = list(biases) + [swap(biases[2], 1)]
        b_qkv = [jnp.concatenate([b[:local_rows].astype(F32), jnp.zeros((local_rows,), F32),
                                  b[local_rows:2 * local_rows].astype(F32)])[:, None] for b in biases]
        b_one = [b[2 * local_rows:] for b in biases]
        w_one_sent = send(w_1)
        core, chip = lax.rem(me, 2), lax.div(me, 2)
        d_here = lax.dynamic_slice_in_dim(d_out, 2 * chip, 2, 0)
        d_there = lax.dynamic_slice_in_dim(d_out, 2 - 2 * chip, 2, 0)
        d_here_near, d_here_two = swap(d_here, 1), swap(d_there, 2)
        w_two_sent = send(w_2)
        d_there_near, d_there_two = swap(d_there, 1), swap(d_here, 2)

        def rows_of(pairs, which):
            return jnp.concatenate([lax.dynamic_index_in_dim(p, which, 0, keepdims=False) for p in pairs], axis=0)

        x_f32 = x_img.astype(F32)
        h_one_f, ln1_pull = jax.vjp(layer_norm, x_f32, ln1_gain, ln1_bias)
        h_one = h_one_f.astype(BF16)
        qkv, mixed, lse = [], [], []
        w_qkv = list(w_qkv_sent[:2])
        for k in range(4):
            if k == 2:
                w_qkv = land(w_qkv_sent, mixed[1])
            block = (dot_nt(w_qkv[k], h_one) + b_qkv[k]).astype(BF16)
            out, stat = attn_fwd(block)
            qkv.append(block)
            mixed.append(out)
            lse.append(stat)
        w_out = land(w_out_sent, mixed[2])
        attn_out = dot_tn(jnp.concatenate(mixed, axis=0), jnp.concatenate(w_out, axis=0))
        x_mid = (x_f32 + attn_out + b_o).astype(BF16)
        mid_f32 = x_mid.astype(F32)
        h_two_f, ln2_pull = jax.vjp(layer_norm, mid_f32, ln2_gain, ln2_bias)
        h_two = h_two_f.astype(BF16)
        h_sent = send(h_two)

        pre, hid = [], []
        w_one = list(w_one_sent[:2])
        for k in range(4):
            if k == 2:
                w_one = land(w_one_sent, hid[1])
            u = (dot(h_two, w_one[k]) + b_one[k]).astype(BF16)
            pre.append(u)
            hid.append(gelu_tanh(u.astype(F32)).astype(BF16))

        def pull_gelu(u, d_g):
            _, pull = jax.vjp(gelu_tanh, u.astype(F32))
            return pull(d_g.astype(F32))[0].astype(BF16)

        def own_columns(h_rows, d_rows):
            u = (dot(h_rows, w_1) + b_1).astype(BF16)
            g = gelu_tanh(u.astype(F32)).astype(BF16)
            d_u = pull_gelu(u, dot_nt(d_rows, w_2).astype(BF16))
            return h_rows, d_rows, g, d_u

        d_here_two, _ = lax.optimization_barrier((d_here_two, hid[3]))
        d_here_diag = swap(d_here_two, 1)
        d_img = rows_of((d_here, d_here_near, d_here_two, d_here_diag), core)
        d_sib = rows_of((d_here_near, d_here, d_here_diag, d_here_two), 1 - core)
        w_two = list(w_two_sent[:2])
        d_pre = [pull_gelu(pre[k], dot_nt(d_img, w_two[k]).astype(BF16)) for k in range(2)]
        part_sib = own_columns(h_sent[1], d_sib)
        w_two = land(w_two_sent, (part_sib[3], d_pre[1]))
        d_pre += [pull_gelu(pre[k], dot_nt(d_img, w_two[k]).astype(BF16)) for k in (2, 3)]
        mlp_out = dot(hid[0], w_two[0])
        for k in range(1, 4):
            mlp_out += dot(hid[k], w_two[k])
        y_img = (mid_f32 + mlp_out + b_2).astype(BF16)
        y_out = to_tokens(y_img)

        d_h_two_f = dot_nt(d_pre[0], w_one[0])
        for k in range(1, 4):
            d_h_two_f += dot_nt(d_pre[k], w_one[k])
        d_h_two = d_h_two_f.astype(BF16)
        d_mid_ln, g_ln2_gain, g_ln2_bias = ln2_pull(d_h_two.astype(F32))
        d_mid = (d_img.astype(F32) + d_mid_ln).astype(BF16)

        def reduce_cross(part):
            return swap(part[2] + swap(part[3], 1), 2)

        def reduce_near(part, crossed):
            return part[0] + swap(part[1], 1) + crossed

        g_o_part = [dot(mixed[k], d_mid) for k in range(4)]
        g_w_o = reduce_near(g_o_part, reduce_cross(g_o_part))
        d_qkv, g_qkv_part = [None] * 4, [None] * 4
        for k in (3, 2, 1, 0):
            d_mixed = dot_nt(w_out[k], d_mid).astype(BF16)
            d_qkv[k] = attn_bwd(qkv[k], d_mixed, lse[k])
            g_qkv_part[k] = dot(d_qkv[k], h_one)
        g_w_qkv = reduce_near(g_qkv_part, reduce_cross(g_qkv_part)).astype(BF16)
        g_w_q, g_w_k, g_w_v = [g_w_qkv[i * local_rows:(i + 1) * local_rows].T.reshape(w_q.shape) for i in range(3)]

        d_h_one = dot_tn(jnp.concatenate(d_qkv, axis=0), jnp.concatenate(w_qkv, axis=0)).astype(BF16)
        h_all = land(h_sent, d_h_one)
        d_there_two, _ = lax.optimization_barrier((d_there_two, d_mid))
        d_there_diag = swap(d_there_two, 1)
        d_far = jnp.concatenate([rows_of((d_there_two, d_there_diag, d_there, d_there_near), core),
                                 rows_of((d_there_diag, d_there_two, d_there_near, d_there), 1 - core)], axis=0)
        parts = [(h_two, d_img, hid[0], d_pre[0]), part_sib, own_columns(jnp.concatenate(h_all[2:], axis=0), d_far)]
        g_w_1 = sum(dot_tn(h_rows, d_u) for h_rows, _, _, d_u in parts).astype(BF16)
        g_w_2 = sum(dot_tn(g, d_rows) for _, d_rows, g, _ in parts).astype(BF16)
        g_b_1 = sum(jnp.sum(d_u, axis=0, dtype=F32) for _, _, _, d_u in parts).astype(BF16)
        d_in_ln, g_ln1_gain, g_ln1_bias = ln1_pull(d_h_one.astype(F32))
        grad_x_img = (d_mid.astype(F32) + d_in_ln).astype(BF16)
        grad_x = to_tokens(grad_x_img)

        b_part = [jnp.sum(d, axis=1, dtype=F32) for d in d_qkv]
        g_b_qkv = reduce_near(b_part, reduce_cross(b_part)).astype(BF16)
        vecs = jnp.stack([g_ln1_gain, g_ln1_bias, jnp.sum(d_mid, axis=0, dtype=F32), g_ln2_gain, g_ln2_bias,
                          jnp.sum(d_img, axis=0, dtype=F32)])
        vecs = vecs + swap(vecs, 1)
        vecs = vecs + swap(vecs, 2)
        return (y_out, grad_x, vecs[0], vecs[1], g_w_q, g_b_qkv[:local_rows].reshape(b_q.shape), g_w_k, g_w_v,
                g_b_qkv[2 * local_rows:].reshape(b_v.shape), g_w_o.astype(BF16).reshape(w_o.shape),
                vecs[2].astype(BF16), vecs[3], vecs[4], g_w_1, g_b_1, g_w_2, vecs[5].astype(BF16))

    return jax.shard_map(layer_step, mesh=mesh, in_specs=in_specs, out_specs=out_specs, check_vma=False)
```

time: 1240 us -> 721 us (0.58)
  waiting for transfers between devices: 678 us -> 177 us
  matrix products: 450 us -> 285 us
  Pallas kernels: 0 us -> 122 us
  local copies, waits for them, and re-layouts: 8.37 us -> 57 us
  other arithmetic: 73.2 us -> 42 us
  starting transfers between devices: 0.5 us -> 25.5 us
  between operations: 14.9 us -> 2.08 us
    reduce_scatter x4 -> x0, waiting for transfers between devices: 440 us -> none  [scatter_sum(): return lax.psum_scatter(part_sum, 'tp', scatter_dimension=1, tiled=True)]
    all_gather x4 -> x0, waiting for transfers between devices: 237 us -> none  [gather_tokens(): return lax.all_gather(local_rows, 'tp', axis=1, tiled=True)]
    ppermute x0 -> x44, waiting for transfers between devices: none -> 177 us  [swap(): return lax.ppermute(value, 'tp', [(i, i ^ k) for i in range(4)])]
    pallas_call x0 -> x8, Pallas kernels: none -> 122 us  [the longest x4 62.8 us: attn_bwd(): pl.pallas_call(attn_bwd_kernel, grid=(pairs,), in_specs=[spec(0), spec(1)...]
    dot_general x23 -> x42, matrix products: 376 us -> 285 us  [the longest x16 118 us: dot_nt(): lax.dot_general(a, b, (((1,), (1,)), ((), ())), preferred_element_type=F32)]
    sub x2 -> x0, matrix products: 74.8 us -> none  [attention_core(): probs = jax.nn.softmax(scores, axis=-1).astype(jnp.bfloat16)]
    convert_element_type x9 -> x8, other arithmetic: 42.7 us -> 11.4 us  [the longest x1 4.07 us: layer_step(): grad_x_img = (d_mid.astype(F32) + d_in_ln).astype(BF16)]
    ppermute x0 -> x44, starting transfers between devices: none -> 25.5 us  [swap(): return lax.ppermute(value, 'tp', [(i, i ^ k) for i in range(4)])]
  transfers between devices with their start and end apart: 8 -> 44, of which waited for: 8 -> 9; matrix products, arithmetic and copies ran while one was open for 9% -> 52% of each run, Pallas kernels for 0% -> 17%
where the time goes in v1:
time: 721 us; the launch traced here: 710 us
  matrix products  285 us (40%)
  waiting for transfers between devices  177 us (25%)
  Pallas kernels  122 us (17%)
  local copies, waits for them, and re-layouts  57 us (8%)
  other arithmetic  42 us (6%)
  starting transfers between devices  25.5 us (4%)
    ppermute x44, waiting for transfers between devices, swap(): return lax.ppermute(value, 'tp', [(i, i ^ k) for i in range(4)])  177 us
    dot_general x16, matrix products, dot_nt(): lax.dot_general(a, b, (((1,), (1,)), ((), ())), preferred_element_type=F32)  118 us
    dot_general x18, matrix products, dot(): return jnp.dot(a, b, preferred_element_type=F32)  102 us
    dot_general x8, matrix products, dot_tn(): lax.dot_general(a, b, (((0,), (0,)), ((), ())), preferred_element_type=F32)  65 us
    pallas_call x4, Pallas kernels, attn_bwd(): pl.pallas_call(attn_bwd_kernel, grid=(pairs,), in_specs=[spec(0), spec(1)...  62.8 us
    pallas_call x4, Pallas kernels, attn_fwd(): pl.pallas_call(attn_fwd_kernel, grid=(pairs,), in_specs=[spec(0), spec(1)...  59.5 us
    ppermute x44, starting transfers between devices, swap(): return lax.ppermute(value, 'tp', [(i, i ^ k) for i in range(4)])  25.5 us
    unnamed x175, local copies, waits for them, and re-layouts  20.5 us
  transfers between devices with their start and end apart: 44, of which 9 were waited for; matrix products, arithmetic and copies ran while one was open for 52% of the time, Pallas kernels for 17%

profile of v1, /device:TPU:0, one launch (start us, length us, event | category | flops | bytes accessed | tf_op | source)
XLA Modules:
  0.0 710.3 jit_solution(17978678088931507580)
XLA Ops:
  25.8 41.0 %collective-permute-done.2 = bf16[256,1152]{1,0:T(8,128)(2,1)S(1)} collective-permute-done((bf16[256,1152]{1,0:T(8,128)(2,1)}, bf16[256,1152]{1,0:T(8,128)(2,1)S(1)}, u32[]{:S(2)}, u32[]{:S(2)}) %collective-permute-start.2) | collective-permute-done | bytes 589856 | tf_op jit(solution)/shard_map/ppermute | solution.py:156
  68.0 13.0 %collective-permute-done.1 = bf16[256,1152]{1,0:T(8,128)(2,1)S(1)} collective-permute-done((bf16[256,1152]{1,0:T(8,128)(2,1)}, bf16[256,1152]{1,0:T(8,128)(2,1)S(1)}, u32[]{:S(2)}, u32[]{:S(2)}) %collective-permute-start.1) | collective-permute-done | bytes 589856 | tf_op jit(solution)/shard_map/ppermute | solution.py:156
  95.1 14.7 %attn_fwd.5 = (bf16[288,1024]{1,0:T(8,128)(2,1)}, f32[2,8,1024]{2,1,0:T(8,128)}) custom-call(bf16[864,1024]{1,0:T(8,128)(2,1)} %add_convert_fusion.4.q_ref.k_ref.v_ref, bf16[864,1024]{1,0:T(8,128)(2,1)} %add_convert_fusion.4.q_ref.k_ref.v_ref, bf16[864,1024]{1,0:T(8,128)(2,1)} %add_convert_fusion.4.q_ref.k_ref.v_ref), custom_call_target="tpu_custom_call" | custom-call | flops 4831838208 | bytes 2359296 | tf_op jit(solution)/shard_map/attn_fwd/pallas_call | solution.py:111
  110.3 14.9 %attn_fwd.4 = (bf16[288,1024]{1,0:T(8,128)(2,1)}, f32[2,8,1024]{2,1,0:T(8,128)}) custom-call(bf16[864,1024]{1,0:T(8,128)(2,1)} %add_convert_fusion.5.q_ref.k_ref.v_ref, bf16[864,1024]{1,0:T(8,128)(2,1)} %add_convert_fusion.5.q_ref.k_ref.v_ref, bf16[864,1024]{1,0:T(8,128)(2,1)} %add_convert_fusion.5.q_ref.k_ref.v_ref), custom_call_target="tpu_custom_call" | custom-call | flops 4831838208 | bytes 2359296 | tf_op jit(solution)/shard_map/attn_fwd/pallas_call | solution.py:111
  133.2 15.1 %attn_fwd.6 = (bf16[288,1024]{1,0:T(8,128)(2,1)}, f32[2,8,1024]{2,1,0:T(8,128)}) custom-call(bf16[864,1024]{1,0:T(8,128)(2,1)} %add_convert_fusion.3.q_ref.k_ref.v_ref, bf16[864,1024]{1,0:T(8,128)(2,1)} %add_convert_fusion.3.q_ref.k_ref.v_ref, bf16[864,1024]{1,0:T(8,128)(2,1)} %add_convert_fusion.3.q_ref.k_ref.v_ref), custom_call_target="tpu_custom_call" | custom-call | flops 4831838208 | bytes 2359296 | tf_op jit(solution)/shard_map/attn_fwd/pallas_call | solution.py:111
  162.1 14.8 %attn_fwd.7 = (bf16[288,1024]{1,0:T(8,128)(2,1)}, f32[2,8,1024]{2,1,0:T(8,128)}) custom-call(bf16[864,1024]{1,0:T(8,128)(2,1)} %add_convert_fusion.2.q_ref.k_ref.v_ref, bf16[864,1024]{1,0:T(8,128)(2,1)} %add_convert_fusion.2.q_ref.k_ref.v_ref, bf16[864,1024]{1,0:T(8,128)(2,1)} %add_convert_fusion.2.q_ref.k_ref.v_ref), custom_call_target="tpu_custom_call" | custom-call | flops 4831838208 | bytes 2359296 | tf_op jit(solution)/shard_map/attn_fwd/pallas_call | solution.py:111
  213.3 8.2 %fusion.97 = (bf16[1024,1076]{0,1:T(8,128)(2,1)}, f32[1024,1076]{0,1:T(8,128)}) fusion(f32[1076]{0:T(1024)S(1)} %copy-done.61, bf16[1024,1152]{1,0:T(8,128)(2,1)} %fusion.40, bf16[1152,1076]{0,1:T(8,128)(2,1)S(1)} %collective-permute-done.18), kind=kOutput, calls=%fused_computation.162 | convolution fusion | flops 2551824384 | bytes 11453648 | tf_op jit(solution)/shard_map/dot_general | solution.py:30
  221.5 33.9 %collective-permute-done.17 = bf16[2,256,1152]{2,1,0:T(8,128)(2,1)S(1)} collective-permute-done((bf16[2,256,1152]{2,1,0:T(8,128)(2,1)S(1)}, bf16[2,256,1152]{2,1,0:T(8,128)(2,1)S(1)}, u32[]{:S(2)}, u32[]{:S(2)}) %collective-permute-start.17) | collective-permute-done | bytes 1179680 | tf_op jit(solution)/shard_map/ppermute | solution.py:156
  269.0 9.9 %convert_reduce_fusion.8 = (f32[1076]{0:T(1024)}, bf16[1024,1076]{0,1:T(8,128)(2,1)S(1)}) fusion(bf16[1024,1076]{0,1:T(8,128)(2,1)S(1)} %fusion.111, bf16[1076,1152]{1,0:T(8,128)(2,1)} %param.32, bf16[256,1152]{1,0:T(8,128)(2,1)S(1)} %get-tuple-element.98, bf16[256,1152]{1,0:T(8,128)(2,1)S(1)} %get-tuple-element.96, bf16[256,1152]{1,0:T(8,128)(2,1)S(1)} %copy-done.25, ...), kind=kOutput, calls=%fused_computation.172 | convolution fusion | flops 2575584256 | bytes 9250000 | tf_op jit(solution)/shard_map/dot_general | solution.py:34
  289.5 9.1 %fusion.61 = bf16[1024,1076]{0,1:T(8,128)(2,1)S(1)} fusion(bf16[1024,1076]{0,1:T(8,128)(2,1)S(1)} %fusion.112, bf16[1076,1152]{1,0:T(8,128)(2,1)} %collective-permute-done.13, bf16[256,1152]{1,0:T(8,128)(2,1)S(1)} %get-tuple-element.98, bf16[256,1152]{1,0:T(8,128)(2,1)S(1)} %get-tuple-element.96, bf16[256,1152]{1,0:T(8,128)(2,1)S(1)} %copy-done.25, ...), kind=kOutput, calls=%fused_computation.126 | convolution fusion | flops 2573381632 | bytes 9245696 | tf_op jit(solution)/shard_map/dot_general | solution.py:34
  313.2 10.0 %convert_reduce_fusion.7 = (f32[1076]{0:T(1024)}, bf16[1024,1076]{0,1:T(8,128)(2,1)S(1)}) fusion(bf16[1024,1076]{0,1:T(8,128)(2,1)S(1)} %fusion.114, bf16[1076,1152]{1,0:T(8,128)(2,1)} %param.32, bf16[256,1152]{1,0:T(8,128)(2,1)S(1)} %get-tuple-element.97, bf16[256,1152]{1,0:T(8,128)(2,1)S(1)} %get-tuple-element.99, bf16[256,1152]{1,0:T(8,128)(2,1)S(1)} %copy-done.38, ...), kind=kOutput, calls=%fused_computation.171 | convolution fusion | flops 2575584256 | bytes 9250000 | tf_op jit(solution)/shard_map/dot_general | solution.py:34
  341.5 14.0 %fusion.150 = f32[1024,1152]{1,0:T(8,128)} fusion(bf16[1152,1076]{0,1:T(8,128)(2,1)} %collective-permute-done.14, bf16[1024,1076]{0,1:T(8,128)(2,1)} %copy-done.76, bf16[1076,1152]{1,0:T(8,128)(2,1)} %collective-permute-done.15, bf16[256,1152]{1,0:T(8,128)(2,1)} %copy-done.28, bf16[256,1152]{1,0:T(8,128)(2,1)} %copy-done.26, ...), kind=kOutput, calls=%fused_computation.243 | convolution fusion | flops 5111984128 | bytes 14239744 | tf_op jit(solution)/shard_map/dot_general | solution.py:34
  355.5 17.8 %convert_reduce_fusion.2 = (f32[1152]{0:T(1024)}, f32[1024]{0:T(1024)S(1)}, bf16[1024,1152]{1,0:T(8,128)(2,1)}) fusion(f32[1152]{0:T(1024)} %param.28, f32[1024]{0:T(1024)S(1)} %broadcast_multiply_fusion, bf16[1024,1152]{1,0:T(8,128)(2,1)S(1)} %get-tuple-element.113, bf16[1152,1076]{0,1:T(8,128)(2,1)} %copy-done.69, ...), kind=kOutput, calls=%fused_computation.65 | convolution fusion | flops 5127161856 | bytes 30620880 | tf_op jit(solution)/shard_map/dot_general | solution.py:34
  373.3 13.7 %fusion.53 = (f32[1152]{0:T(1024)}, f32[1024]{0:T(1024)S(1)}, bf16[1024,1152]{1,0:T(8,128)(2,1)}) fusion(bf16[1024,1152]{1,0:T(8,128)(2,1)} %get-tuple-element.116, bf16[1024,1152]{1,0:T(8,128)(2,1)S(1)} %get-tuple-element.113, f32[1024]{0:T(1024)S(1)} %copy-done.47, f32[1024]{0:T(1024)S(1)} %broadcast_multiply_fusion, ...), kind=kOutput, calls=%fused_computation.114 | convolution fusion | flops 2559834112 | bytes 25946624 | tf_op jit(solution)/shard_map/dot_general | solution.py:30
  400.1 15.8 %attn_bwd.7 = bf16[3,288,1024]{2,1,0:T(8,128)(2,1)} custom-call(bf16[864,1024]{1,0:T(8,128)(2,1)} %add_convert_fusion.2.q_ref.k_ref.v_ref, bf16[864,1024]{1,0:T(8,128)(2,1)} %add_convert_fusion.2.q_ref.k_ref.v_ref, bf16[864,1024]{1,0:T(8,128)(2,1)} %add_convert_fusion.2.q_ref.k_ref.v_ref, bf16[288,1024]{1,0:T(8,128)(2,1)} %convolution_convert_fusion.6.g_ref, ...), custom_call_target="tpu_custom_call" | custom-call | flops 12079595520 | bytes 4718592 | tf_op jit(solution)/shard_map/attn_bwd/pallas_call | solution.py:128
  415.9 15.7 %attn_bwd.6 = bf16[3,288,1024]{2,1,0:T(8,128)(2,1)} custom-call(bf16[864,1024]{1,0:T(8,128)(2,1)} %add_convert_fusion.3.q_ref.k_ref.v_ref, bf16[864,1024]{1,0:T(8,128)(2,1)} %add_convert_fusion.3.q_ref.k_ref.v_ref, bf16[864,1024]{1,0:T(8,128)(2,1)} %add_convert_fusion.3.q_ref.k_ref.v_ref, bf16[288,1024]{1,0:T(8,128)(2,1)} %convolution_convert_fusion.7.g_ref, ...), custom_call_target="tpu_custom_call" | custom-call | flops 12079595520 | bytes 4718592 | tf_op jit(solution)/shard_map/attn_bwd/pallas_call | solution.py:128
  434.5 15.5 %attn_bwd.5 = bf16[3,288,1024]{2,1,0:T(8,128)(2,1)} custom-call(bf16[864,1024]{1,0:T(8,128)(2,1)} %add_convert_fusion.4.q_ref.k_ref.v_ref, bf16[864,1024]{1,0:T(8,128)(2,1)} %add_convert_fusion.4.q_ref.k_ref.v_ref, bf16[864,1024]{1,0:T(8,128)(2,1)} %add_convert_fusion.4.q_ref.k_ref.v_ref, bf16[288,1024]{1,0:T(8,128)(2,1)} %fusion.152.g_ref, ...), custom_call_target="tpu_custom_call" | custom-call | flops 12079595520 | bytes 4718592 | tf_op jit(solution)/shard_map/attn_bwd/pallas_call | solution.py:128
  450.1 15.8 %attn_bwd.4 = bf16[3,288,1024]{2,1,0:T(8,128)(2,1)} custom-call(bf16[864,1024]{1,0:T(8,128)(2,1)} %add_convert_fusion.5.q_ref.k_ref.v_ref, bf16[864,1024]{1,0:T(8,128)(2,1)} %add_convert_fusion.5.q_ref.k_ref.v_ref, bf16[864,1024]{1,0:T(8,128)(2,1)} %add_convert_fusion.5.q_ref.k_ref.v_ref, bf16[288,1024]{1,0:T(8,128)(2,1)} %fusion.151.g_ref, ...), custom_call_target="tpu_custom_call" | custom-call | flops 12079595520 | bytes 4718592 | tf_op jit(solution)/shard_map/attn_bwd/pallas_call | solution.py:128
  466.0 18.4 %convert_reduce_fusion.1 = (f32[1152]{0:T(1024)}, f32[1024]{0:T(1024)S(1)}, bf16[1024,1152]{1,0:T(8,128)(2,1)S(1)}) fusion(f32[1152]{0:T(1024)S(1)} %copy-done.43, f32[1024]{0:T(1024)S(1)} %copy-done.41, bf16[256,1152]{1,0:T(8,128)(2,1)S(1)} %copy-done.3, bf16[256,1152]{1,0:T(8,128)(2,1)S(1)} %copy-done.5, bf16[256,1152]{1,0:T(8,128)(2,1)S(1)} %copy-done.7, ...), kind=kOutput, calls=%fused_computation.61 | convolution fusion | flops 8199731200 | bytes 19776512 | tf_op jit(solution)/shard_map/dot_general | solution.py:38
  543.0 10.7 %collective-permute-done.29 = f32[6,1152]{1,0:T(8,128)} collective-permute-done((f32[6,1152]{1,0:T(8,128)}, f32[6,1152]{1,0:T(8,128)}, u32[]{:S(2)}, u32[]{:S(2)}) %collective-permute-start.29) | collective-permute-done | bytes 27680 | tf_op jit(solution)/shard_map/ppermute | solution.py:156
  595.3 15.4 %convert_reduce_fusion = (f32[1076]{0:T(1024)S(1)}, bf16[2048,1076]{0,1:T(8,128)(2,1)}) fusion(bf16[2048,1076]{0,1:T(8,128)(2,1)} %fusion.11, bf16[2048,1152]{1,0:T(8,128)(2,1)S(1)} %bitcast_dynamic-update-slice_fusion, bf16[1076,1152]{1,0:T(8,128)(2,1)} %param.32), kind=kOutput, calls=%fused_computation.22 | convolution fusion | flops 5132295168 | bytes 16016592 | tf_op jit(solution)/shard_map/dot_general | solution.py:34
  618.2 9.6 %fusion.12 = bf16[1152,1076]{0,1:T(8,128)(2,1)} fusion(f32[1152,1076]{0,1:T(8,128)} %convolution_add_fusion.3, bf16[2048,1152]{1,0:T(8,128)(2,1)S(1)} %constant_dynamic-update-slice_fusion.6, bf16[2048,1076]{0,1:T(8,128)(2,1)} %get-tuple-element.119), kind=kOutput, calls=%fused_computation.49 | convolution fusion | flops 5079684096 | bytes 16563200 | tf_op jit(solution)/shard_map/dot_general | solution.py:38
  627.8 10.6 %fusion.13 = bf16[1076,1152]{1,0:T(8,128)(2,1)} fusion(f32[1076,1152]{1,0:T(8,128)} %convolution_add_fusion.2, bf16[2048,1152]{1,0:T(8,128)(2,1)S(1)} %bitcast_dynamic-update-slice_fusion, bf16[2048,1076]{0,1:T(8,128)(2,1)} %fusion.11), kind=kOutput, calls=%fused_computation.50 | convolution fusion | flops 5101720576 | bytes 16563200 | tf_op jit(solution)/shard_map/dot_general | solution.py:38
  641.8 64.1 %collective-permute-done.32 = f32[864,1152]{1,0:T(8,128)S(1)} collective-permute-done((f32[864,1152]{1,0:T(8,128)}, f32[864,1152]{1,0:T(8,128)S(1)}, u32[]{:S(2)}, u32[]{:S(2)}) %collective-permute-start.32) | collective-permute-done | bytes 3981344 | tf_op jit(solution)/shard_map/ppermute | solution.py:156
  (364 shorter events, 286.5 us)
Async XLA Ops:
  9.2 100.6 %collective-permute-start.5 = (bf16[864,1152]{1,0:T(8,128)(2,1)}, bf16[864,1152]{1,0:T(8,128)(2,1)}, u32[]{:S(2)}, u32[]{:S(2)}) collective-permute-start(bf16[864,1152]{1,0:T(8,128)(2,1)} %pad_maximum_fusion.7), channel_id=1, source_target_pairs={{0,2},{1,3},{2,0},{3,1},{4,6},{5,7},{6,4},{7,5},{8,10},{9,11},{10,... | collective-permute-start | bytes 5971976 | tf_op jit(solution)/shard_map/ppermute | solution.py:156
  12.1 54.7 %collective-permute-start.2 = (bf16[256,1152]{1,0:T(8,128)(2,1)}, bf16[256,1152]{1,0:T(8,128)(2,1)S(1)}, u32[]{:S(2)}, u32[]{:S(2)}) collective-permute-start(bf16[256,1152]{1,0:T(8,128)(2,1)} %get-tuple-element.89), channel_id=1, source_target_pairs={{0,3},{1,2},{2,1},{3,0},{4,7},{5,6},{6,5},{7,4},{8,11},{9,10},{10,... | collective-permute-start | bytes 1769480 | tf_op jit(solution)/shard_map/ppermute | solution.py:156
  13.6 67.3 %collective-permute-start.1 = (bf16[256,1152]{1,0:T(8,128)(2,1)}, bf16[256,1152]{1,0:T(8,128)(2,1)S(1)}, u32[]{:S(2)}, u32[]{:S(2)}) collective-permute-start(bf16[256,1152]{1,0:T(8,128)(2,1)} %get-tuple-element.90), channel_id=1, source_target_pairs={{0,2},{1,3},{2,0},{3,1},{4,6},{5,7},{6,4},{7,5},{8,10},{9,11},{10,... | collective-permute-start | bytes 1769480 | tf_op jit(solution)/shard_map/ppermute | solution.py:156
  22.6 58.4 %collective-permute-start = (bf16[256,1152]{1,0:T(8,128)(2,1)}, bf16[256,1152]{1,0:T(8,128)(2,1)S(1)}, u32[]{:S(2)}, u32[]{:S(2)}) collective-permute-start(bf16[256,1152]{1,0:T(8,128)(2,1)} %get-tuple-element.88), channel_id=1, source_target_pairs={{0,1},{1,0},{2,3},{3,2},{4,5},{5,4},{6,7},{7,6},{8,9},{9,8},{10,11... | collective-permute-start | bytes 1769480 | tf_op jit(solution)/shard_map/ppermute | solution.py:156
  24.8 65.4 %collective-permute-start.3 = (bf16[864,1152]{1,0:T(8,128)(2,1)}, bf16[864,1152]{1,0:T(8,128)(2,1)S(1)}, u32[]{:S(2)}, u32[]{:S(2)}) collective-permute-start(bf16[864,1152]{1,0:T(8,128)(2,1)} %pad_maximum_fusion.7), channel_id=1, source_target_pairs={{0,1},{1,0},{2,3},{3,2},{4,5},{5,4},{6,7},{7,6},{8,9},{9,8},{10,11... | collective-permute-start | bytes 5971976 | tf_op jit(solution)/shard_map/ppermute | solution.py:156
  66.8 81.4 %collective-permute-start.10 = (bf16[288,1152]{1,0:T(8,128)(2,1)}, bf16[288,1152]{1,0:T(8,128)(2,1)}, u32[]{:S(2)}, u32[]{:S(2)}) collective-permute-start(bf16[288,1152]{1,0:T(8,128)(2,1)} %bitcast.173), channel_id=1, source_target_pairs={{0,2},{1,3},{2,0},{3,1},{4,6},{5,7},{6,4},{7,5},{8,10},{9,11},{10,... | collective-permute-start | bytes 1990664 | tf_op jit(solution)/shard_map/ppermute | solution.py:156
  81.0 96.0 %collective-permute-start.9 = (bf16[288,1152]{1,0:T(8,128)(2,1)}, bf16[288,1152]{1,0:T(8,128)(2,1)}, u32[]{:S(2)}, u32[]{:S(2)}) collective-permute-start(bf16[288,1152]{1,0:T(8,128)(2,1)} %bitcast.174), channel_id=1, source_target_pairs={{0,1},{1,0},{2,3},{3,2},{4,5},{5,4},{6,7},{7,6},{8,9},{9,8},{10,11... | collective-permute-start | bytes 1990664 | tf_op jit(solution)/shard_map/ppermute | solution.py:156
  81.0 75.4 %collective-permute-start.14 = (bf16[1152,1076]{0,1:T(8,128)(2,1)}, bf16[1152,1076]{0,1:T(8,128)(2,1)}, u32[]{:S(2)}, u32[]{:S(2)}) collective-permute-start(bf16[1152,1076]{0,1:T(8,128)(2,1)} %param.30), channel_id=1, source_target_pairs={{0,2},{1,3},{2,0},{3,1},{4,6},{5,7},{6,4},{7,5},{8,10},{9,11},{10,... | collective-permute-start | bytes 7437320 | tf_op jit(solution)/shard_map/ppermute | solution.py:156
  109.8 46.5 %collective-permute-start.7 = (bf16[864,1152]{1,0:T(8,128)(2,1)}, bf16[864,1152]{1,0:T(8,128)(2,1)}, u32[]{:S(2)}, u32[]{:S(2)}) collective-permute-start(bf16[864,1152]{1,0:T(8,128)(2,1)} %collective-permute-done.5), channel_id=1, source_target_pairs={{0,1},{1,0},{2,3},{3,2},{4,5},{5,4},{6,7},{7,6},{8,9},{9,8},{10,11... | collective-permute-start | bytes 5971976 | tf_op jit(solution)/shard_map/ppermute | solution.py:156
  125.2 80.3 %collective-permute-start.12 = (bf16[1152,1076]{0,1:T(8,128)(2,1)}, bf16[1152,1076]{0,1:T(8,128)(2,1)}, u32[]{:S(2)}, u32[]{:S(2)}) collective-permute-start(bf16[1152,1076]{0,1:T(8,128)(2,1)} %param.30), channel_id=1, source_target_pairs={{0,1},{1,0},{2,3},{3,2},{4,5},{5,4},{6,7},{7,6},{8,9},{9,8},{10,11... | collective-permute-start | bytes 7437320 | tf_op jit(solution)/shard_map/ppermute | solution.py:156
  148.2 175.0 %collective-permute-start.15 = (bf16[1076,1152]{1,0:T(8,128)(2,1)}, bf16[1076,1152]{1,0:T(8,128)(2,1)}, u32[]{:S(2)}, u32[]{:S(2)}) collective-permute-start(bf16[1076,1152]{1,0:T(8,128)(2,1)} %param.32), channel_id=1, source_target_pairs={{0,2},{1,3},{2,0},{3,1},{4,6},{5,7},{6,4},{7,5},{8,10},{9,11},{10,... | collective-permute-start | bytes 7437320 | tf_op jit(solution)/shard_map/ppermute | solution.py:156
  156.3 102.2 %collective-permute-start.13 = (bf16[1076,1152]{1,0:T(8,128)(2,1)}, bf16[1076,1152]{1,0:T(8,128)(2,1)}, u32[]{:S(2)}, u32[]{:S(2)}) collective-permute-start(bf16[1076,1152]{1,0:T(8,128)(2,1)} %param.32), channel_id=1, source_target_pairs={{0,1},{1,0},{2,3},{3,2},{4,5},{5,4},{6,7},{7,6},{8,9},{9,8},{10,11... | collective-permute-start | bytes 7437320 | tf_op jit(solution)/shard_map/ppermute | solution.py:156
  176.9 343.9 %collective-permute-start.41 = (bf16[2,256,1152]{2,1,0:T(8,128)(2,1)}, bf16[2,256,1152]{2,1,0:T(8,128)(2,1)}, u32[]{:S(2)}, u32[]{:S(2)}) collective-permute-start(bf16[2,256,1152]{2,1,0:T(8,128)(2,1)} %get-tuple-element.85), channel_id=1, source_target_pairs={{0,2},{1,3},{2,0},{3,1},{4,6},{5,7},{6,4},{7,5},{8,10},{9,11},{10,... | collective-permute-start | bytes 3538952 | tf_op jit(solution)/shard_map/ppermute | solution.py:156
  205.6 49.9 %collective-permute-start.17 = (bf16[2,256,1152]{2,1,0:T(8,128)(2,1)S(1)}, bf16[2,256,1152]{2,1,0:T(8,128)(2,1)S(1)}, u32[]{:S(2)}, u32[]{:S(2)}) collective-permute-start(bf16[2,256,1152]{2,1,0:T(8,128)(2,1)S(1)} %copy-done.37), channel_id=1, source_target_pairs={{0,2},{1,3},{2,0},{3,1},{4,6},{5,7},{6,4},{7,5},{8,10},{9,11},{10,... | collective-permute-start | bytes 3538952 | tf_op jit(solution)/shard_map/ppermute | solution.py:156
  213.1 92.5 %collective-permute-start.20 = (bf16[1024,1152]{1,0:T(8,128)(2,1)}, bf16[1024,1152]{1,0:T(8,128)(2,1)S(1)}, u32[]{:S(2)}, u32[]{:S(2)}) collective-permute-start(bf16[1024,1152]{1,0:T(8,128)(2,1)} %fusion.40), channel_id=1, source_target_pairs={{0,1},{1,0},{2,3},{3,2},{4,5},{5,4},{6,7},{7,6},{8,9},{9,8},{10,11... | collective-permute-start | bytes 7077896 | tf_op jit(solution)/shard_map/ppermute | solution.py:156
  258.5 245.1 %collective-permute-start.39 = (bf16[1024,1152]{1,0:T(8,128)(2,1)}, bf16[1024,1152]{1,0:T(8,128)(2,1)}, u32[]{:S(2)}, u32[]{:S(2)}) collective-permute-start(bf16[1024,1152]{1,0:T(8,128)(2,1)} %fusion.40), channel_id=1, source_target_pairs={{0,2},{1,3},{2,0},{3,1},{4,6},{5,7},{6,4},{7,5},{8,10},{9,11},{10,... | collective-permute-start | bytes 7077896 | tf_op jit(solution)/shard_map/ppermute | solution.py:156
  494.1 62.1 %collective-permute-start.27 = (bf16[256,1152]{1,0:T(8,128)(2,1)}, bf16[256,1152]{1,0:T(8,128)(2,1)}, u32[]{:S(2)}, u32[]{:S(2)}) collective-permute-start(bf16[256,1152]{1,0:T(8,128)(2,1)} %get-tuple-element.71), channel_id=1, source_target_pairs={{0,3},{1,2},{2,1},{3,0},{4,7},{5,6},{6,5},{7,4},{8,11},{9,10},{10,... | collective-permute-start | bytes 1769480 | tf_op jit(solution)/shard_map/ppermute | solution.py:156
  494.3 63.3 %collective-permute-start.26 = (bf16[256,1152]{1,0:T(8,128)(2,1)}, bf16[256,1152]{1,0:T(8,128)(2,1)}, u32[]{:S(2)}, u32[]{:S(2)}) collective-permute-start(bf16[256,1152]{1,0:T(8,128)(2,1)} %get-tuple-element.72), channel_id=1, source_target_pairs={{0,2},{1,3},{2,0},{3,1},{4,6},{5,7},{6,4},{7,5},{8,10},{9,11},{10,... | collective-permute-start | bytes 1769480 | tf_op jit(solution)/shard_map/ppermute | solution.py:156
  496.0 62.1 %collective-permute-start.25 = (bf16[256,1152]{1,0:T(8,128)(2,1)}, bf16[256,1152]{1,0:T(8,128)(2,1)}, u32[]{:S(2)}, u32[]{:S(2)}) collective-permute-start(bf16[256,1152]{1,0:T(8,128)(2,1)} %get-tuple-element.73), channel_id=1, source_target_pairs={{0,1},{1,0},{2,3},{3,2},{4,5},{5,4},{6,7},{7,6},{8,9},{9,8},{10,11... | collective-permute-start | bytes 1769480 | tf_op jit(solution)/shard_map/ppermute | solution.py:156
  568.6 42.7 %collective-permute-start.31 = (f32[864,1152]{1,0:T(8,128)}, f32[864,1152]{1,0:T(8,128)}, u32[]{:S(2)}, u32[]{:S(2)}) collective-permute-start(f32[864,1152]{1,0:T(8,128)} %fusion.202), channel_id=1, source_target_pairs={{0,1},{1,0},{2,3},{3,2},{4,5},{5,4},{6,7},{7,6},{8,9},{9,8},{10,11... | collective-permute-start | bytes 11943944 | tf_op jit(solution)/shard_map/ppermute | solution.py:156
  568.6 73.2 %collective-permute-start.30 = (f32[864,1152]{1,0:T(8,128)S(1)}, f32[864,1152]{1,0:T(8,128)S(1)}, u32[]{:S(2)}, u32[]{:S(2)}) collective-permute-start(f32[864,1152]{1,0:T(8,128)S(1)} %copy-done.66), channel_id=1, source_target_pairs={{0,1},{1,0},{2,3},{3,2},{4,5},{5,4},{6,7},{7,6},{8,9},{9,8},{10,11... | collective-permute-start | bytes 11943944 | tf_op jit(solution)/shard_map/ppermute | solution.py:156
  576.3 62.2 %collective-permute-start.36 = (f32[288,1152]{1,0:T(8,128)S(1)}, f32[288,1152]{1,0:T(8,128)}, u32[]{:S(2)}, u32[]{:S(2)}) collective-permute-start(f32[288,1152]{1,0:T(8,128)S(1)} %copy-done.70), channel_id=1, source_target_pairs={{0,1},{1,0},{2,3},{3,2},{4,5},{5,4},{6,7},{7,6},{8,9},{9,8},{10,11... | collective-permute-start | bytes 3981320 | tf_op jit(solution)/shard_map/ppermute | solution.py:156
  585.3 53.1 %collective-permute-start.38 = (f32[288,1152]{1,0:T(8,128)}, f32[288,1152]{1,0:T(8,128)S(1)}, u32[]{:S(2)}, u32[]{:S(2)}) collective-permute-start(f32[288,1152]{1,0:T(8,128)} %convolution_add_fusion.11), channel_id=1, source_target_pairs={{0,2},{1,3},{2,0},{3,1},{4,6},{5,7},{6,4},{7,5},{8,10},{9,11},{10,... | collective-permute-start | bytes 3981320 | tf_op jit(solution)/shard_map/ppermute | solution.py:156
  617.9 88.0 %collective-permute-start.32 = (f32[864,1152]{1,0:T(8,128)}, f32[864,1152]{1,0:T(8,128)S(1)}, u32[]{:S(2)}, u32[]{:S(2)}) collective-permute-start(f32[864,1152]{1,0:T(8,128)} %convolution_add_fusion.9), channel_id=1, source_target_pairs={{0,2},{1,3},{2,0},{3,1},{4,6},{5,7},{6,4},{7,5},{8,10},{9,11},{10,... | collective-permute-start | bytes 11943944 | tf_op jit(solution)/shard_map/ppermute | solution.py:156
  (101 other events, 1981.6 us)

commit v2 on v1

v2 whole, which is shorter than its diff:
```python
import math
import jax
import jax.numpy as jnp
from jax import lax
from jax.experimental import pallas as pl
from jax.experimental.pallas import tpu as pltpu
from jax.sharding import PartitionSpec as P

LN_EPS = 1e-6
HEAD = 72
PAIR = 2 * HEAD
FWD_QUERIES = 1024
BWD_QUERIES = 512
ROWS = 512
GELU_C = math.sqrt(2.0 / math.pi)
F32 = jnp.float32
BF16 = jnp.bfloat16
LOG2E = 1.4426950408889634


def layer_norm(rows, ln_gain, ln_bias):
    row_mean = jnp.mean(rows, axis=-1, keepdims=True)
    centered = rows - row_mean
    variance = jnp.mean(centered * centered, axis=-1, keepdims=True)
    return centered * lax.rsqrt(variance + LN_EPS) * ln_gain + ln_bias


def dot(a, b):
    return jnp.dot(a, b, preferred_element_type=F32)


def dot_nt(a, b):
    return lax.dot_general(a, b, (((1,), (1,)), ((), ())), preferred_element_type=F32)


def dot_tn(a, b):
    return lax.dot_general(a, b, (((0,), (0,)), ((), ())), preferred_element_type=F32)


def attn_fwd_kernel(w_ref, b_ref, h_ref, qkv_ref, o_ref, l_ref):
    tokens = h_ref.shape[1]
    coef = LOG2E / math.sqrt(HEAD)
    parts = [(dot(w_ref[i], h_ref[...]) + b_ref[i]).astype(BF16) for i in range(3)]
    for i in range(3):
        qkv_ref[i] = parts[i]
    q_all, k_all, v_all = [part.astype(F32) for part in parts]
    keys = [k_all[h * HEAD:(h + 1) * HEAD].T.astype(BF16) for h in range(2)]
    vals = [v_all[h * HEAD:(h + 1) * HEAD].astype(BF16) for h in range(2)]
    quer = [q_all[h * HEAD:(h + 1) * HEAD].astype(BF16) for h in range(2)]
    for start in range(0, tokens, FWD_QUERIES):
        outs = []
        for h in range(2):
            s = dot(keys[h], quer[h][:, start:start + FWD_QUERIES])
            top = jnp.max(s, axis=0, keepdims=True)
            e = jnp.exp2((s - top) * coef)
            total = jnp.sum(e, axis=0, keepdims=True)
            p = (e * (1.0 / total)).astype(BF16)
            outs.append(dot(vals[h], p))
            l_ref[0, h:h + 1, start:start + FWD_QUERIES] = top * coef + jnp.log2(total)
        o_ref[:, start:start + FWD_QUERIES] = jnp.concatenate(outs, axis=0).astype(BF16)


def attn_bwd_kernel(qkv_ref, g_ref, l_ref, h_ref, d_ref, gw_ref, gb_ref, dk_acc, dv_acc):
    tokens = h_ref.shape[0]
    scale = 1.0 / math.sqrt(HEAD)
    coef = LOG2E * scale
    q_all, k_all, v_all = [qkv_ref[i].astype(F32) for i in range(3)]
    g_all = g_ref[...].astype(F32)

    def head(a, h):
        return a[h * HEAD:(h + 1) * HEAD]

    k_t = [head(k_all, h).astype(BF16) for h in range(2)]
    keys = [head(k_all, h).T.astype(BF16) for h in range(2)]
    vals = [head(v_all, h).T.astype(BF16) for h in range(2)]
    q_t = [head(q_all, h).astype(BF16) for h in range(2)]
    q_n = [head(q_all, h).T.astype(BF16) for h in range(2)]
    g_t = [head(g_all, h).astype(BF16) for h in range(2)]
    g_n = [head(g_all, h).T.astype(BF16) for h in range(2)]
    for start in range(0, tokens, BWD_QUERIES):
        cols = slice(start, start + BWD_QUERIES)
        dqs = []
        for h in range(2):
            s = dot(keys[h], q_t[h][:, cols])
            p = jnp.exp2(s * coef - l_ref[0, h:h + 1, cols])
            dp = dot(vals[h], g_t[h][:, cols]).astype(BF16).astype(F32)
            delta = jnp.sum(p * dp, axis=0, keepdims=True)
            ds = (p * ((dp - delta) * scale)).astype(BF16)
            dv = dot(p.astype(BF16), g_n[h][cols])
            dk = dot(ds, q_n[h][cols])
            if start == 0:
                dv_acc[h] = dv
                dk_acc[h] = dk
            else:
                dv_acc[h] += dv
                dk_acc[h] += dk
            dqs.append(dot(k_t[h], ds))
        d_ref[0, :, cols] = jnp.concatenate(dqs, axis=0).astype(BF16)
    d_ref[1] = jnp.concatenate([dk_acc[h].T for h in range(2)], axis=0).astype(BF16)
    d_ref[2] = jnp.concatenate([dv_acc[h].T for h in range(2)], axis=0).astype(BF16)
    ones = jnp.ones((8, tokens), BF16)
    for i in range(3):
        gw_ref[i] = dot(d_ref[i], h_ref[...])
        gb_ref[i, 0] = dot_nt(ones, d_ref[i])


def attn_fwd(w, bias, h_one):
    _, rows, width = w.shape
    tokens = h_one.shape[1]
    pairs = rows // PAIR
    flops = 16 * rows * tokens * tokens + 6 * rows * tokens * width
    trio = lambda c: pl.BlockSpec((3, PAIR, c), lambda i: (0, i, 0))
    return pl.pallas_call(
        attn_fwd_kernel,
        grid=(pairs,),
        in_specs=[trio(width), trio(1), pl.BlockSpec((width, tokens), lambda i: (0, 0), pipeline_mode=pl.Buffered(1))],
        out_specs=[trio(tokens), pl.BlockSpec((PAIR, tokens), lambda i: (i, 0)),
                   pl.BlockSpec((1, 8, tokens), lambda i: (i, 0, 0))],
        out_shape=[jax.ShapeDtypeStruct((3, rows, tokens), BF16), jax.ShapeDtypeStruct((rows, tokens), BF16),
                   jax.ShapeDtypeStruct((pairs, 8, tokens), F32)],
        cost_estimate=pl.CostEstimate(flops=flops, bytes_accessed=14 * rows * tokens, transcendentals=0),
        name="af",
    )(w, bias, h_one)


def attn_bwd(qkv, d_mixed, lse, h_one):
    _, rows, tokens = qkv.shape
    width = h_one.shape[1]
    pairs = rows // PAIR
    flops = 40 * rows * tokens * tokens + 6 * rows * tokens * width
    trio = lambda c: pl.BlockSpec((3, PAIR, c), lambda i: (0, i, 0))
    return pl.pallas_call(
        attn_bwd_kernel,
        grid=(pairs,),
        in_specs=[trio(tokens), pl.BlockSpec((PAIR, tokens), lambda i: (i, 0)), pl.BlockSpec((1, 8, tokens), lambda i: (i, 0, 0)),
                  pl.BlockSpec((tokens, width), lambda i: (0, 0), pipeline_mode=pl.Buffered(1))],
        out_specs=[trio(tokens), trio(width), pl.BlockSpec((3, 1, 8, PAIR), lambda i: (0, i, 0, 0))],
        out_shape=[jax.ShapeDtypeStruct((3, rows, tokens), BF16), jax.ShapeDtypeStruct((3, rows, width), F32),
                   jax.ShapeDtypeStruct((3, pairs, 8, PAIR), F32)],
        scratch_shapes=[pltpu.VMEM((2, tokens, HEAD), F32), pltpu.VMEM((2, tokens, HEAD), F32)],
        cost_estimate=pl.CostEstimate(flops=flops, bytes_accessed=30 * rows * tokens, transcendentals=0),
        name="ab",
    )(qkv, d_mixed, lse, h_one)


def gelu_and_slope(pre_act):
    square = pre_act * pre_act
    bend = jnp.tanh(GELU_C * pre_act * (1.0 + 0.044715 * square))
    half = 0.5 * (1.0 + bend)
    slope = half + 0.5 * pre_act * (1.0 - bend * bend) * (GELU_C * (1.0 + 3 * 0.044715 * square))
    return pre_act * half, slope


def mlp_in_kernel(h_ref, wa_ref, wb_ref, ba_ref, bb_ref, ua_ref, ub_ref):
    ua_ref[...] = (dot_nt(h_ref[...], wa_ref[...]) + ba_ref[...]).astype(BF16)
    ub_ref[...] = (dot_nt(h_ref[...], wb_ref[...]) + bb_ref[...]).astype(BF16)


def mlp_block(u_ref, d_ref, w1_ref, w2_ref):
    g, slope = gelu_and_slope(u_ref[...].astype(F32))
    g = g.astype(BF16)
    d_g = dot_nt(d_ref[...], w2_ref[...]).astype(BF16).astype(F32)
    d_u = (d_g * slope).astype(BF16)
    return g, d_u, dot(g, w2_ref[...]), dot(d_u, w1_ref[...])


def add_row_sum(sum_ref, rows):
    part = dot(jnp.ones((8, rows.shape[0]), BF16), rows)[:1] if rows.dtype == BF16 else jnp.sum(rows, axis=0, keepdims=True)

    @pl.when(pl.program_id(0) == 0)
    def _():
        sum_ref[...] = part

    @pl.when(pl.program_id(0) > 0)
    def _():
        sum_ref[...] += part


def mlp_near_kernel(ua_ref, ub_ref, d_ref, w1a_ref, w1b_ref, w2a_ref, w2b_ref, g_ref, du_ref, y_ref, dh_ref, dus_ref, ds_ref):
    g, d_u, y, d_h = mlp_block(ua_ref, d_ref, w1a_ref, w2a_ref)
    g_ref[...] = g
    du_ref[...] = d_u
    add_row_sum(dus_ref, d_u)
    add_row_sum(ds_ref, d_ref[...])
    _, _, y_b, d_h_b = mlp_block(ub_ref, d_ref, w1b_ref, w2b_ref)
    y_ref[...] = y + y_b
    dh_ref[...] = d_h + d_h_b


def norm_bwd_tile(x_ref, d_h, res_ref, gain_ref, out_ref, dgain_ref, dbias_ref, dout_ref):
    x = x_ref[...].astype(F32)
    centered = x - jnp.mean(x, axis=-1, keepdims=True)
    inv = lax.rsqrt(jnp.mean(centered * centered, axis=-1, keepdims=True) + LN_EPS)
    unit = centered * inv
    add_row_sum(dbias_ref, d_h)
    d_h = d_h.astype(F32)
    d_unit = d_h * gain_ref[...]
    tilt = jnp.mean(d_unit * unit, axis=-1, keepdims=True)
    d_x = inv * (d_unit - jnp.mean(d_unit, axis=-1, keepdims=True) - unit * tilt)
    out = (res_ref[...].astype(F32) + d_x).astype(BF16)
    out_ref[...] = out
    add_row_sum(dgain_ref, d_h * unit)
    if dout_ref is not None:
        add_row_sum(dout_ref, out)


def norm_one_kernel(*refs):
    d_refs, (x_ref, res_ref), w_refs, rest = refs[:4], refs[4:6], refs[6:10], refs[10:]
    d_h = dot_tn(d_refs[0][...], w_refs[0][...])
    for d_ref, w_ref in zip(d_refs[1:], w_refs[1:]):
        d_h += dot_tn(d_ref[...], w_ref[...])
    gain_ref, out_ref, dgain_ref, dbias_ref = rest
    norm_bwd_tile(x_ref, d_h.astype(BF16), res_ref, gain_ref, out_ref, dgain_ref, dbias_ref, None)


def norm_one_bwd(d_qkv, w_qkv, x, residual, gain):
    tokens, width = x.shape
    tile = 256
    rows = pl.BlockSpec((tile, width), lambda i: (i, 0))
    whole = lambda op: pl.BlockSpec(op.shape, lambda i: (0, 0), pipeline_mode=pl.Buffered(1))
    depth = d_qkv[0].shape[0]
    return pl.pallas_call(
        norm_one_kernel,
        grid=(tokens // tile,),
        in_specs=[pl.BlockSpec((depth, tile), lambda i: (0, i))] * 4 + [rows, rows] + [whole(w) for w in w_qkv] + [whole(gain)],
        out_specs=[rows] + [pl.BlockSpec((1, width), lambda i: (0, 0))] * 2,
        out_shape=[jax.ShapeDtypeStruct((tokens, width), BF16)] + [jax.ShapeDtypeStruct((1, width), F32)] * 2,
        cost_estimate=pl.CostEstimate(flops=8 * depth * tokens * width, bytes_accessed=30 * depth * tokens, transcendentals=0),
        name="nob",
    )(*d_qkv, x, residual, *w_qkv, gain)


def mlp_far_kernel(ua_ref, ub_ref, d_ref, w1a_ref, w1b_ref, w2a_ref, w2b_ref, x_ref, b_ref, gain_ref, yp_ref, dhp_ref,
                   y_ref, out_ref, dgain_ref, dbias_ref, dout_ref):
    _, _, y, d_h = mlp_block(ua_ref, d_ref, w1a_ref, w2a_ref)
    _, _, y_b, d_h_b = mlp_block(ub_ref, d_ref, w1b_ref, w2b_ref)
    y_ref[...] = (x_ref[...].astype(F32) + (yp_ref[...] + (y + y_b)) + b_ref[...]).astype(BF16)
    d_h = (dhp_ref[...] + (d_h + d_h_b)).astype(BF16)
    norm_bwd_tile(x_ref, d_h, d_ref, gain_ref, out_ref, dgain_ref, dbias_ref, dout_ref)


def mlp_own_kernel(h_ref, d_ref, w1_ref, w2_ref, b_ref, g_ref, du_ref, dus_ref):
    u = (dot_nt(h_ref[...], w1_ref[...]) + b_ref[...]).astype(BF16)
    g, slope = gelu_and_slope(u.astype(F32))
    g_ref[...] = g.astype(BF16)
    d_g = dot_nt(d_ref[...], w2_ref[...]).astype(BF16).astype(F32)
    d_u = (d_g * slope).astype(BF16)
    du_ref[...] = d_u
    add_row_sum(dus_ref, d_u)


def row_call(kernel, tiled, fixed, outs, flops, order=None, sums=(), tile=ROWS):
    rows = tiled[0].shape[0]
    operands = tiled + fixed if order is None else [(tiled + fixed)[i] for i in order]
    is_tiled = [True] * len(tiled) + [False] * len(fixed)
    is_tiled = is_tiled if order is None else [is_tiled[i] for i in order]
    in_specs = [pl.BlockSpec((tile, op.shape[1]), lambda i: (i, 0)) if t
                else pl.BlockSpec(op.shape, lambda i: (0, 0), pipeline_mode=pl.Buffered(1))
                for op, t in zip(operands, is_tiled)]
    size = sum(op.size * op.dtype.itemsize for op in operands) + sum(rows * c * d.dtype.itemsize for c, d in
                                                                     [(c, jnp.zeros((), d)) for c, d in outs])
    return pl.pallas_call(
        kernel,
        grid=(rows // tile,),
        in_specs=in_specs,
        out_specs=[pl.BlockSpec((tile, c), lambda i: (i, 0)) for c, _ in outs] + [pl.BlockSpec((1, c), lambda i: (0, 0)) for c in sums],
        out_shape=[jax.ShapeDtypeStruct((rows, c), d) for c, d in outs] + [jax.ShapeDtypeStruct((1, c), F32) for c in sums],
        cost_estimate=pl.CostEstimate(flops=flops, bytes_accessed=size, transcendentals=0),
    )(*operands)


def solution(mesh):
    act_spec = P('dp', 'tp', None)
    replicated = P()
    head_w = P(None, 'tp', None)
    head_b = P('tp', None)
    grad_head_w = P('dp', 'tp', None)
    grad_head_b = P(('dp', 'tp'), None)
    grad_vec = P('dp')
    in_specs = (act_spec, act_spec, replicated, replicated, head_w, head_b, head_w, head_w, head_b,
                P('tp', None, None), replicated, replicated, replicated, P(None, 'tp'), P('tp'), P('tp', None), replicated)
    out_specs = (act_spec, act_spec, grad_vec, grad_vec, grad_head_w, grad_head_b, grad_head_w, grad_head_w, grad_head_b,
                 P(('dp', 'tp'), None, None), grad_vec, grad_vec, grad_vec, P('dp', 'tp'), P(('dp', 'tp')),
                 P(('dp', 'tp'), None), grad_vec)

    def swap(value, k):
        return lax.ppermute(value, 'tp', [(i, i ^ k) for i in range(4)])

    def send(block):
        return block, swap(block, 1), swap(block, 2)

    def land(sent, dep):
        own, near, two = sent
        two, _ = lax.optimization_barrier((two, dep))
        return [own, near, two, swap(two, 1)]

    def layer_step(x, d_out, ln1_gain, ln1_bias, w_q, b_q, w_k, w_v, b_v, w_o, b_o, ln2_gain, ln2_bias, w_1, b_1, w_2, b_2):
        me = lax.axis_index('tp')
        width = x.shape[2]
        slab = x.shape[1]
        local_rows = w_o.shape[0] * w_o.shape[1]

        def image(shard, k):
            return lax.dynamic_index_in_dim(shard, me ^ k, 0, keepdims=False)

        def to_image(shard):
            return jnp.concatenate([image(shard, 0)] + [swap(image(shard, k), k) for k in (1, 2, 3)], axis=0)

        def to_tokens(rows):
            parts = [rows[:slab]] + [swap(rows[k * slab:(k + 1) * slab], k) for k in (1, 2, 3)]
            stacked = jnp.stack(parts)
            return jnp.stack([lax.dynamic_index_in_dim(stacked, me ^ i, 0, keepdims=False) for i in range(4)])

        x_img = to_image(x)
        w_qkv_own = jnp.stack([w.reshape(width, local_rows).T for w in (w_q, w_k, w_v)])
        w_qkv_sent = send(w_qkv_own)
        w_out_sent = send(w_o.reshape(local_rows, width))
        bias_own = jnp.concatenate([b_q.reshape(-1).astype(F32), b_v.reshape(-1).astype(F32), b_1.astype(F32)])
        biases = send(bias_own)
        biases = list(biases) + [swap(biases[2], 1)]
        b_qkv = [jnp.stack([b[:local_rows], jnp.zeros((local_rows,), F32), b[local_rows:2 * local_rows]])[:, :, None]
                 for b in biases]
        b_one = [b[2 * local_rows:] for b in biases]
        w_one_own = w_1.T
        w_one_sent = send(w_one_own)
        core, chip = lax.rem(me, 2), lax.div(me, 2)
        d_here = lax.dynamic_slice_in_dim(d_out, 2 * chip, 2, 0)
        d_there = lax.dynamic_slice_in_dim(d_out, 2 - 2 * chip, 2, 0)
        d_here_near, d_here_two = swap(d_here, 1), swap(d_there, 2)
        w_two_sent = send(w_2)
        d_there_near, d_there_two = swap(d_there, 1), swap(d_here, 2)

        def rows_of(pairs, which):
            return jnp.concatenate([lax.dynamic_index_in_dim(p, which, 0, keepdims=False) for p in pairs], axis=0)

        x_f32 = x_img.astype(F32)
        h_one = layer_norm(x_f32, ln1_gain, ln1_bias).astype(BF16)
        h_one_t = lax.optimization_barrier(h_one.T)
        qkv, mixed, lse = [], [], []
        w_qkv = list(w_qkv_sent[:2])
        for k in range(4):
            if k == 2:
                w_qkv = land(w_qkv_sent, mixed[1])
            block, out, stat = attn_fwd(w_qkv[k], b_qkv[k], h_one_t)
            qkv.append(block)
            mixed.append(out)
            lse.append(stat)
        w_out = land(w_out_sent, mixed[2])
        attn_out = dot_tn(jnp.concatenate(mixed, axis=0), jnp.concatenate(w_out, axis=0))
        x_mid = (x_f32 + attn_out + b_o).astype(BF16)
        mid_f32 = x_mid.astype(F32)
        h_two = layer_norm(mid_f32, ln2_gain, ln2_bias).astype(BF16)
        h_sent = send(h_two)

        cols = w_1.shape[1]
        mm = 2 * h_two.shape[0] * width * cols
        b_one = [b[None, :] for b in b_one]

        def mlp_in(w, b):
            return row_call(mlp_in_kernel, [h_two], [*w, *b], [(cols, BF16)] * 2, 2 * mm)

        pre_near = mlp_in(w_one_sent[:2], b_one[:2])

        def own_columns(h_rows, d_rows):
            g, d_u, d_u_sum = row_call(mlp_own_kernel, [h_rows, d_rows], [w_one_own, w_2, b_one[0]], [(cols, BF16)] * 2,
                                       2 * mm * (h_rows.shape[0] // h_two.shape[0]), sums=(cols,))
            return h_rows, d_rows, g, d_u, d_u_sum

        d_here_two, _ = lax.optimization_barrier((d_here_two, pre_near[1]))
        d_here_diag = swap(d_here_two, 1)
        d_img = rows_of((d_here, d_here_near, d_here_two, d_here_diag), core)
        d_sib = rows_of((d_here_near, d_here, d_here_diag, d_here_two), 1 - core)
        g_own, d_u_own, y_part, d_h_part, d_u_sum, d_sum = row_call(
            mlp_near_kernel, [*pre_near, d_img], [*w_one_sent[:2], *w_two_sent[:2]],
            [(cols, BF16)] * 2 + [(width, F32)] * 2, 6 * mm, sums=(cols, width))
        part_sib = own_columns(h_sent[1], d_sib)
        w_one = land(w_one_sent, (part_sib[3], y_part))
        pre_far = mlp_in(w_one[2:], b_one[2:])
        parts = [(h_two, d_img, g_own, d_u_own, d_u_sum), part_sib]
        g_w_1 = sum(dot_tn(p[3], p[0]) for p in parts)
        g_w_2 = sum(dot_tn(p[2], p[1]) for p in parts)
        g_w_1, g_w_2 = lax.optimization_barrier((g_w_1, g_w_2))
        w_two = land(w_two_sent, pre_far[1])
        y_img, d_mid, g_ln2_gain, g_ln2_bias, d_mid_sum = row_call(
            mlp_far_kernel, [*pre_far, d_img, x_mid, y_part, d_h_part],
            [*w_one[2:], *w_two[2:], b_2.astype(F32)[None, :], ln2_gain[None, :]], [(width, BF16)] * 2, 6 * mm,
            order=(0, 1, 2, 6, 7, 8, 9, 3, 10, 11, 4, 5), sums=(width,) * 3)
        y_out = to_tokens(y_img)

        def reduce_cross(part):
            return swap(part[2] + swap(part[3], 1), 2)

        def reduce_near(part, crossed):
            return part[0] + swap(part[1], 1) + crossed

        g_o_part = [dot(mixed[k], d_mid) for k in range(4)]
        g_w_o = reduce_near(g_o_part, reduce_cross(g_o_part))
        d_qkv, g_qkv_part, b_part = [None] * 4, [None] * 4, [None] * 4
        for k in (3, 2, 1, 0):
            d_mixed = dot_nt(w_out[k], d_mid).astype(BF16)
            d_qkv[k], g_qkv_part[k], b_part[k] = attn_bwd(qkv[k], d_mixed, lse[k], h_one)
        g_w_qkv = reduce_near(g_qkv_part, reduce_cross(g_qkv_part)).astype(BF16)
        g_w_q, g_w_k, g_w_v = [g_w_qkv[i].T.reshape(w_q.shape) for i in range(3)]

        grad_x_img, g_ln1_gain, g_ln1_bias = norm_one_bwd(
            [d.reshape(-1, d.shape[2]) for d in d_qkv], [w.reshape(-1, width) for w in w_qkv], x_img, d_mid, ln1_gain[None, :])
        h_all = land(h_sent, grad_x_img)
        d_there_two, _ = lax.optimization_barrier((d_there_two, d_mid))
        d_there_diag = swap(d_there_two, 1)
        d_far = jnp.concatenate([rows_of((d_there_two, d_there_diag, d_there, d_there_near), core),
                                 rows_of((d_there_diag, d_there_two, d_there_near, d_there), 1 - core)], axis=0)
        part_far = own_columns(jnp.concatenate(h_all[2:], axis=0), d_far)
        g_w_1 = (g_w_1 + dot_tn(part_far[3], part_far[0])).astype(BF16).T
        g_w_2 = (g_w_2 + dot_tn(part_far[2], part_far[1])).astype(BF16)
        g_b_1 = (parts[0][4] + parts[1][4] + part_far[4])[0].astype(BF16)
        grad_x = to_tokens(grad_x_img)

        b_part = [b[:, :, 0] for b in b_part]
        g_b_qkv = reduce_near(b_part, reduce_cross(b_part)).astype(BF16)
        vecs = jnp.concatenate([g_ln1_gain, g_ln1_bias, d_mid_sum, g_ln2_gain, g_ln2_bias, d_sum], axis=0)
        vecs = vecs + swap(vecs, 1)
        vecs = vecs + swap(vecs, 2)
        return (y_out, grad_x, vecs[0], vecs[1], g_w_q, g_b_qkv[0].reshape(b_q.shape), g_w_k, g_w_v,
                g_b_qkv[2].reshape(b_v.shape), g_w_o.astype(BF16).reshape(w_o.shape),
                vecs[2].astype(BF16), vecs[3], vecs[4], g_w_1, g_b_1, g_w_2, vecs[5].astype(BF16))

    return jax.shard_map(layer_step, mesh=mesh, in_specs=in_specs, out_specs=out_specs, check_vma=False)
```

time: 721 us -> 642 us (0.89)
  matrix products: 285 us -> 71.6 us
  Pallas kernels: 122 us -> 265 us
  other arithmetic: 42 us -> 33.4 us
    pallas_call x8 -> x15, Pallas kernels: 122 us -> 265 us  [the longest x6 121 us: row_call(): pl.pallas_call(kernel, grid=(rows // tile,), in_specs=in_specs, out_specs...]
    dot_general x16 -> x4, matrix products: 118 us -> 12.4 us  [dot_nt(): lax.dot_general(a, b, (((1,), (1,)), ((), ())), preferred_element_type=F32)]
    dot_general x18 -> x4, matrix products: 102 us -> 9.45 us  [dot(): return jnp.dot(a, b, preferred_element_type=F32)]
    dot_general x8 -> x7, matrix products: 65 us -> 49.7 us  [dot_tn(): lax.dot_general(a, b, (((0,), (0,)), ((), ())), preferred_element_type=F32)]
    reduce_sum x6 -> x0, other arithmetic: 13.8 us -> none  [the longest x1 4.91 us: layer_step(): jnp.sum(d_mid, axis=0, dtype=F32)]
    broadcast_in_dim x0 -> x11, local copies, waits for them, and re-layouts: none -> 11.5 us  [the longest x4 5.93 us: layer_step(): jnp.stack([b[:local_rows], jnp.zeros((local_rows,), F32), b[local_rows:2...]
    unnamed x175 -> x139, local copies, waits for them, and re-layouts: 20.5 us -> 10.4 us
  transfers between devices with their start and end apart: 44 -> 44, of which waited for: 9 -> 11; matrix products, arithmetic and copies ran while one was open for 52% -> 23% of each run, Pallas kernels for 17% -> 42%
where the time goes in v2:
time: 642 us; the launch traced here: 634 us
  Pallas kernels  265 us (41%)
  waiting for transfers between devices  181 us (28%)
  matrix products  71.6 us (11%)
  local copies, waits for them, and re-layouts  57.6 us (9%)
  other arithmetic  33.4 us (5%)
  starting transfers between devices  23.2 us (4%)
    ppermute x44, waiting for transfers between devices, swap(): return lax.ppermute(value, 'tp', [(i, i ^ k) for i in range(4)])  181 us
    pallas_call x6, Pallas kernels, row_call(): pl.pallas_call(kernel, grid=(rows // tile,), in_specs=in_specs, out_specs...  121 us
    pallas_call x4, Pallas kernels, attn_bwd(): pl.pallas_call(attn_bwd_kernel, grid=(pairs,), in_specs=[trio(tokens), pl...  73.2 us
    pallas_call x4, Pallas kernels, attn_fwd(): pl.pallas_call(attn_fwd_kernel, grid=(pairs,), in_specs=[trio(width), tri...  49.9 us
    dot_general x7, matrix products, dot_tn(): lax.dot_general(a, b, (((0,), (0,)), ((), ())), preferred_element_type=F32)  49.7 us
    ppermute x44, starting transfers between devices, swap(): return lax.ppermute(value, 'tp', [(i, i ^ k) for i in range(4)])  23.2 us
    pallas_call x1, Pallas kernels, norm_one_bwd(): pl.pallas_call(norm_one_kernel, grid=(tokens // tile,), in_specs=[pl.Bloc...  20.5 us
  transfers between devices with their start and end apart: 44, of which 11 were waited for; matrix products, arithmetic and copies ran while one was open for 23% of the time, Pallas kernels for 42%

profile of v2, /device:TPU:0, one launch (start us, length us, event | category | flops | bytes accessed | tf_op | source)
XLA Modules:
  0.0 633.7 jit_solution(2282195581268487527)
XLA Ops:
  26.2 10.7 %collective-permute-done.2 = bf16[256,1152]{1,0:T(8,128)(2,1)S(1)} collective-permute-done((bf16[256,1152]{1,0:T(8,128)(2,1)S(1)}, bf16[256,1152]{1,0:T(8,128)(2,1)S(1)}, u32[]{:S(2)}, u32[]{:S(2)}) %collective-permute-start.2) | collective-permute-done | bytes 589856 | tf_op jit(solution)/shard_map/ppermute | solution.py:287
  47.3 12.3 %af.5 = (bf16[3,288,1024]{2,1,0:T(8,128)(2,1)}, bf16[288,1024]{1,0:T(8,128)(2,1)}, f32[2,8,1024]{2,1,0:T(8,128)}) custom-call(bf16[3,288,1152]{2,1,0:T(8,128)(2,1)} %collective-permute-done.3.w_ref, f32[3,288,1]{2,1,0:T(8,128)} %copy.76.b_ref, bf16[1152,1024]{1,0:T(8,128)(2,1)} %copy.75.h_ref), custom_call_target="tpu_custom_call" | custom-call | flops 6870269952 | bytes 4128768 | tf_op jit(solution)/shard_map/af/pallas_call | solution.py:113
  59.7 21.0 %collective-permute-done.5.w_ref = bf16[3,288,1152]{2,1,0:T(8,128)(2,1)} collective-permute-done((bf16[3,288,1152]{2,1,0:T(8,128)(2,1)}, bf16[3,288,1152]{2,1,0:T(8,128)(2,1)}, u32[]{:S(2)}, u32[]{:S(2)}) %collective-permute-start.5) | collective-permute-done | bytes 1990688 | tf_op jit(solution)/shard_map/ppermute | solution.py:287
  92.9 12.8 %af.6 = (bf16[3,288,1024]{2,1,0:T(8,128)(2,1)}, bf16[288,1024]{1,0:T(8,128)(2,1)}, f32[2,8,1024]{2,1,0:T(8,128)}) custom-call(bf16[3,288,1152]{2,1,0:T(8,128)(2,1)} %collective-permute-done.5.w_ref, f32[3,288,1]{2,1,0:T(8,128)} %copy.78.b_ref, bf16[1152,1024]{1,0:T(8,128)(2,1)} %copy.75.h_ref), custom_call_target="tpu_custom_call" | custom-call | flops 6870269952 | bytes 4128768 | tf_op jit(solution)/shard_map/af/pallas_call | solution.py:113
  105.7 12.3 %af.4 = (bf16[3,288,1024]{2,1,0:T(8,128)(2,1)}, bf16[288,1024]{1,0:T(8,128)(2,1)}, f32[2,8,1024]{2,1,0:T(8,128)}) custom-call(bf16[3,288,1152]{2,1,0:T(8,128)(2,1)} %pad_maximum_fusion.7.w_ref, f32[3,288,1]{2,1,0:T(8,128)} %copy.74.b_ref, bf16[1152,1024]{1,0:T(8,128)(2,1)} %copy.75.h_ref), custom_call_target="tpu_custom_call" | custom-call | flops 6870269952 | bytes 4128768 | tf_op jit(solution)/shard_map/af/pallas_call | solution.py:113
  118.6 12.5 %af.7 = (bf16[3,288,1024]{2,1,0:T(8,128)(2,1)}, bf16[288,1024]{1,0:T(8,128)(2,1)}, f32[2,8,1024]{2,1,0:T(8,128)}) custom-call(bf16[3,288,1152]{2,1,0:T(8,128)(2,1)} %collective-permute-done.7.w_ref, f32[3,288,1]{2,1,0:T(8,128)} %copy.80.b_ref, bf16[1152,1024]{1,0:T(8,128)(2,1)} %copy.75.h_ref), custom_call_target="tpu_custom_call" | custom-call | flops 6870269952 | bytes 4128768 | tf_op jit(solution)/shard_map/af/pallas_call | solution.py:113
  140.7 10.9 %shard_map.296 = (bf16[1024,1076]{1,0:T(8,128)(2,1)}, bf16[1024,1076]{1,0:T(8,128)(2,1)}) custom-call(bf16[1024,1152]{1,0:T(8,128)(2,1)} %fusion.14.h_ref, bf16[1076,1152]{1,0:T(8,128)(2,1)} %bitcast.167, bf16[1076,1152]{1,0:T(8,128)(2,1)} %collective-permute-done.16.wb_ref.w1b_ref, f32[1,1076]{1,0:T(1,128)} %broadcast_in_dim.48.ba_ref.b_ref, ...), custom_call_target="tpu_custom_call" | custom-call | flops 5077204992 | bytes 11733408 | tf_op jit(solution)/shard_map/pallas_call | solution.py:262
  162.3 31.7 %shard_map.298 = (bf16[1024,1076]{1,0:T(8,128)(2,1)}, bf16[1024,1076]{1,0:T(8,128)(2,1)}, f32[1024,1152]{1,0:T(8,128)}, f32[1024,1152]{1,0:T(8,128)}, f32[1,1076]{1,0:T(1,128)}, /*index=5*/f32[1,1152]{1,0:T(1,128)}) custom-call(bf16[1024,1076]{1,0:T(8,128)(2,1)} %get-tuple-element.83.ua_ref, bf16[1024,1076]{1,0:T(8,128)(2,1)} %get-tuple-element.80.ub_ref, ...), custom_call_target="tpu_custom_call" | custom-call | flops 15231614976 | bytes 30527488 | tf_op jit(solution)/shard_map/pallas_call | solution.py:262
  194.1 12.4 %shard_map.297 = (bf16[1024,1076]{1,0:T(8,128)(2,1)}, bf16[1024,1076]{1,0:T(8,128)(2,1)}, f32[1,1076]{1,0:T(1,128)}) custom-call(bf16[1024,1152]{1,0:T(8,128)(2,1)} %collective-permute-done.13.h_ref, bf16[1024,1152]{1,0:T(8,128)(2,1)} %pad_maximum_fusion.1.d_ref, bf16[1076,1152]{1,0:T(8,128)(2,1)} %bitcast.170, bf16[1076,1152]{1,0:T(8,128)(2,1)} %w2_ref.3, ...), custom_call_target="tpu_custom_call" | custom-call | flops 5077204992 | bytes 14088400 | tf_op jit(solution)/shard_map/pallas_call | solution.py:262
  219.8 11.3 %shard_map.299 = (bf16[1024,1076]{1,0:T(8,128)(2,1)}, bf16[1024,1076]{1,0:T(8,128)(2,1)}) custom-call(bf16[1024,1152]{1,0:T(8,128)(2,1)} %fusion.14.h_ref, bf16[1076,1152]{1,0:T(8,128)(2,1)} %collective-permute-done.12.wa_ref.w1a_ref, bf16[1076,1152]{1,0:T(8,128)(2,1)} %collective-permute-done.19.wb_ref.w1b_ref, f32[1,1076]{1,0:T(1,128)} %broadcast_in_dim.50.ba_ref, ...), custom_call_target="tpu_custom_call" | custom-call | flops 5077204992 | bytes 11733408 | tf_op jit(solution)/shard_map/pallas_call | solution.py:262
  231.1 34.5 %collective-permute-done.20.w2a_ref = bf16[1076,1152]{1,0:T(8,128)(2,1)} collective-permute-done((bf16[1076,1152]{1,0:T(8,128)(2,1)}, bf16[1076,1152]{1,0:T(8,128)(2,1)}, u32[]{:S(2)}, u32[]{:S(2)}) %collective-permute-start.20) | collective-permute-done | bytes 2479136 | tf_op jit(solution)/shard_map/ppermute | solution.py:287
  286.6 35.4 %shard_map.300 = (bf16[1024,1152]{1,0:T(8,128)(2,1)}, bf16[1024,1152]{1,0:T(8,128)(2,1)}, f32[1,1152]{1,0:T(1,128)}, f32[1,1152]{1,0:T(1,128)}, f32[1,1152]{1,0:T(1,128)}) custom-call(bf16[1024,1076]{1,0:T(8,128)(2,1)} %get-tuple-element.86.ua_ref, bf16[1024,1076]{1,0:T(8,128)(2,1)} %get-tuple-element.87.ub_ref, bf16[1024,1152]{1,0:T(8,128)(2,1)} %pad_maximum_fusion.2.d_ref, ...), custom_call_target="tpu_custom_call" | custom-call | flops 15231614976 | bytes 33207296 | tf_op jit(solution)/shard_map/pallas_call | solution.py:262
  337.6 18.1 %ab.7 = (bf16[3,288,1024]{2,1,0:T(8,128)(2,1)}, f32[3,288,1152]{2,1,0:T(8,128)}, f32[3,2,8,144]{3,2,1,0:T(8,128)}) custom-call(bf16[3,288,1024]{2,1,0:T(8,128)(2,1)} %get-tuple-element.101.qkv_ref, bf16[288,1024]{1,0:T(8,128)(2,1)} %convolution_convert_fusion.g_ref, f32[2,8,1024]{2,1,0:T(8,128)} %get-tuple-element.102.l_ref, bf16[1024,1152]{1,0:T(8,128)(2,1)} %fusion.10.h_ref), custom_call_target="tpu_custom_call" | custom-call | flops 14118027264 | bytes 8847360 | tf_op jit(solution)/shard_map/ab/pallas_call | solution.py:132
  355.7 18.3 %ab.6 = (bf16[3,288,1024]{2,1,0:T(8,128)(2,1)}, f32[3,288,1152]{2,1,0:T(8,128)}, f32[3,2,8,144]{3,2,1,0:T(8,128)}) custom-call(bf16[3,288,1024]{2,1,0:T(8,128)(2,1)} %get-tuple-element.98.qkv_ref, bf16[288,1024]{1,0:T(8,128)(2,1)} %convolution_convert_fusion.1.g_ref, f32[2,8,1024]{2,1,0:T(8,128)} %get-tuple-element.99.l_ref, bf16[1024,1152]{1,0:T(8,128)(2,1)} %fusion.10.h_ref), custom_call_target="tpu_custom_call" | custom-call | flops 14118027264 | bytes 8847360 | tf_op jit(solution)/shard_map/ab/pallas_call | solution.py:132
  376.8 18.3 %ab.5 = (bf16[3,288,1024]{2,1,0:T(8,128)(2,1)}, f32[3,288,1152]{2,1,0:T(8,128)}, f32[3,2,8,144]{3,2,1,0:T(8,128)}) custom-call(bf16[3,288,1024]{2,1,0:T(8,128)(2,1)} %get-tuple-element.95.qkv_ref, bf16[288,1024]{1,0:T(8,128)(2,1)} %fusion.34.g_ref, f32[2,8,1024]{2,1,0:T(8,128)} %get-tuple-element.96.l_ref, bf16[1024,1152]{1,0:T(8,128)(2,1)} %fusion.10.h_ref), custom_call_target="tpu_custom_call" | custom-call | flops 14118027264 | bytes 8847360 | tf_op jit(solution)/shard_map/ab/pallas_call | solution.py:132
  395.1 18.5 %ab.4 = (bf16[3,288,1024]{2,1,0:T(8,128)(2,1)}, f32[3,288,1152]{2,1,0:T(8,128)}, f32[3,2,8,144]{3,2,1,0:T(8,128)}) custom-call(bf16[3,288,1024]{2,1,0:T(8,128)(2,1)} %get-tuple-element.91.qkv_ref, bf16[288,1024]{1,0:T(8,128)(2,1)} %fusion.33.g_ref, f32[2,8,1024]{2,1,0:T(8,128)} %get-tuple-element.93.l_ref, bf16[1024,1152]{1,0:T(8,128)(2,1)} %fusion.10.h_ref), custom_call_target="tpu_custom_call" | custom-call | flops 14118027264 | bytes 8847360 | tf_op jit(solution)/shard_map/ab/pallas_call | solution.py:132
  413.6 20.5 %nob.1 = (bf16[1024,1152]{1,0:T(8,128)(2,1)}, f32[1,1152]{1,0:T(1,128)}, f32[1,1152]{1,0:T(1,128)}) custom-call(bf16[864,1024]{1,0:T(8,128)(2,1)} %bitcast.175, bf16[864,1024]{1,0:T(8,128)(2,1)} %bitcast.174, bf16[864,1024]{1,0:T(8,128)(2,1)} %bitcast.173, bf16[864,1024]{1,0:T(8,128)(2,1)} %bitcast.172, bf16[1024,1152]{1,0:T(8,128)(2,1)} %copy-done, ...), custom_call_target="tpu_custom_call" | custom-call | flops 8153726976 | bytes 26542080 | tf_op jit(solution)/shard_map/nob/pallas_call | solution.py:222
  452.5 22.4 %collective-permute-done.29 = f32[6,1152]{1,0:T(8,128)} collective-permute-done((f32[6,1152]{1,0:T(8,128)}, f32[6,1152]{1,0:T(8,128)}, u32[]{:S(2)}, u32[]{:S(2)}) %collective-permute-start.29) | collective-permute-done | bytes 27680 | tf_op jit(solution)/shard_map/ppermute | solution.py:287
  480.1 11.2 %collective-permute-done.26 = bf16[256,1152]{1,0:T(8,128)(2,1)S(1)} collective-permute-done((bf16[256,1152]{1,0:T(8,128)(2,1)}, bf16[256,1152]{1,0:T(8,128)(2,1)S(1)}, u32[]{:S(2)}, u32[]{:S(2)}) %collective-permute-start.26) | collective-permute-done | bytes 589856 | tf_op jit(solution)/shard_map/ppermute | solution.py:287
  491.3 10.2 %collective-permute-done.27 = bf16[256,1152]{1,0:T(8,128)(2,1)S(1)} collective-permute-done((bf16[256,1152]{1,0:T(8,128)(2,1)}, bf16[256,1152]{1,0:T(8,128)(2,1)S(1)}, u32[]{:S(2)}, u32[]{:S(2)}) %collective-permute-start.27) | collective-permute-done | bytes 589856 | tf_op jit(solution)/shard_map/ppermute | solution.py:287
  515.5 19.5 %shard_map.301 = (bf16[2048,1076]{1,0:T(8,128)(2,1)}, bf16[2048,1076]{1,0:T(8,128)(2,1)}, f32[1,1076]{1,0:T(1,128)}) custom-call(bf16[2048,1152]{1,0:T(8,128)(2,1)} %constant_dynamic-update-slice_fusion.h_ref, bf16[2048,1152]{1,0:T(8,128)(2,1)} %copy-done.24, bf16[1076,1152]{1,0:T(8,128)(2,1)} %bitcast.171, bf16[1076,1152]{1,0:T(8,128)(2,1)} %w2_ref.3, ...), custom_call_target="tpu_custom_call" | custom-call | flops 10154409984 | bytes 23214288 | tf_op jit(solution)/shard_map/pallas_call | solution.py:262
  540.9 12.3 %fusion.1 = bf16[1076,1152]{1,0:T(8,128)(2,1)} fusion(f32[1076,1152]{1,0:T(8,128)} %convolution_add_fusion.2, bf16[2048,1076]{1,0:T(8,128)(2,1)} %get-tuple-element.130, bf16[2048,1152]{1,0:T(8,128)(2,1)S(1)} %copy-done.25), kind=kOutput, calls=%fused_computation.5 | convolution fusion | flops 5079684096 | bytes 16563200 | tf_op jit(solution)/shard_map/dot_general | solution.py:37
  553.3 10.2 %fusion.2 = bf16[1152,1076]{0,1:T(8,128)(2,1)} fusion(f32[1076,1152]{1,0:T(8,128)S(1)} %bitcast.178, bf16[2048,1076]{1,0:T(8,128)(2,1)S(1)} %bitcast.180, bf16[2048,1152]{1,0:T(8,128)(2,1)} %constant_dynamic-update-slice_fusion.h_ref), kind=kOutput, calls=%fused_computation.9 | convolution fusion | flops 5079684096 | bytes 16563200 | tf_op jit(solution)/shard_map/dot_general | solution.py:37
  566.8 62.5 %collective-permute-done.32 = f32[3,288,1152]{2,1,0:T(8,128)S(1)} collective-permute-done((f32[3,288,1152]{2,1,0:T(8,128)S(1)}, f32[3,288,1152]{2,1,0:T(8,128)S(1)}, u32[]{:S(2)}, u32[]{:S(2)}) %collective-permute-start.32) | collective-permute-done | bytes 3981344 | tf_op jit(solution)/shard_map/ppermute | solution.py:287
  (315 shorter events, 172.0 us)
Async XLA Ops:
  15.7 31.7 %collective-permute-start.3 = (bf16[3,288,1152]{2,1,0:T(8,128)(2,1)}, bf16[3,288,1152]{2,1,0:T(8,128)(2,1)}, u32[]{:S(2)}, u32[]{:S(2)}) collective-permute-start(bf16[3,288,1152]{2,1,0:T(8,128)(2,1)} %pad_maximum_fusion.7.w_ref), channel_id=1, source_target_pairs={{0,1},{1,0},{2,3},{3,2},{4,5},{5,4},{6,7},{7,6},{8,9},{9,8},{10,11... | collective-permute-start | bytes 5971976 | tf_op jit(solution)/shard_map/ppermute | solution.py:287
  20.4 60.2 %collective-permute-start.5 = (bf16[3,288,1152]{2,1,0:T(8,128)(2,1)}, bf16[3,288,1152]{2,1,0:T(8,128)(2,1)}, u32[]{:S(2)}, u32[]{:S(2)}) collective-permute-start(bf16[3,288,1152]{2,1,0:T(8,128)(2,1)} %pad_maximum_fusion.7.w_ref), channel_id=1, source_target_pairs={{0,2},{1,3},{2,0},{3,1},{4,6},{5,7},{6,4},{7,5},{8,10},{9,11},{10,... | collective-permute-start | bytes 5971976 | tf_op jit(solution)/shard_map/ppermute | solution.py:287
  80.7 37.4 %collective-permute-start.7 = (bf16[3,288,1152]{2,1,0:T(8,128)(2,1)}, bf16[3,288,1152]{2,1,0:T(8,128)(2,1)}, u32[]{:S(2)}, u32[]{:S(2)}) collective-permute-start(bf16[3,288,1152]{2,1,0:T(8,128)(2,1)} %collective-permute-done.5.w_ref), channel_id=1, source_target_pairs={{0,1},{1,0},{2,3},{3,2},{4,5},{5,4},{6,7},{7,6},{8,9},{9,8},{10,11... | collective-permute-start | bytes 5971976 | tf_op jit(solution)/shard_map/ppermute | solution.py:287
  80.9 50.1 %collective-permute-start.9 = (bf16[288,1152]{1,0:T(8,128)(2,1)}, bf16[288,1152]{1,0:T(8,128)(2,1)}, u32[]{:S(2)}, u32[]{:S(2)}) collective-permute-start(bf16[288,1152]{1,0:T(8,128)(2,1)} %bitcast.18), channel_id=1, source_target_pairs={{0,1},{1,0},{2,3},{3,2},{4,5},{5,4},{6,7},{7,6},{8,9},{9,8},{10,11... | collective-permute-start | bytes 1990664 | tf_op jit(solution)/shard_map/ppermute | solution.py:287
  81.2 59.6 %collective-permute-start.16 = (bf16[1076,1152]{1,0:T(8,128)(2,1)}, bf16[1076,1152]{1,0:T(8,128)(2,1)}, u32[]{:S(2)}, u32[]{:S(2)}) collective-permute-start(bf16[1076,1152]{1,0:T(8,128)(2,1)} %bitcast.166), channel_id=1, source_target_pairs={{0,1},{1,0},{2,3},{3,2},{4,5},{5,4},{6,7},{7,6},{8,9},{9,8},{10,11... | collective-permute-start | bytes 7437320 | tf_op jit(solution)/shard_map/ppermute | solution.py:287
  84.3 67.4 %collective-permute-start.15 = (bf16[2,256,1152]{2,1,0:T(8,128)(2,1)S(1)}, bf16[2,256,1152]{2,1,0:T(8,128)(2,1)}, u32[]{:S(2)}, u32[]{:S(2)}) collective-permute-start(bf16[2,256,1152]{2,1,0:T(8,128)(2,1)S(1)} %get-tuple-element.160), channel_id=1, source_target_pairs={{0,2},{1,3},{2,0},{3,1},{4,6},{5,7},{6,4},{7,5},{8,10},{9,11},{10,... | collective-permute-start | bytes 3538952 | tf_op jit(solution)/shard_map/ppermute | solution.py:287
  118.1 35.9 %collective-permute-start.14 = (bf16[2,256,1152]{2,1,0:T(8,128)(2,1)}, bf16[2,256,1152]{2,1,0:T(8,128)(2,1)}, u32[]{:S(2)}, u32[]{:S(2)}) collective-permute-start(bf16[2,256,1152]{2,1,0:T(8,128)(2,1)} %get-tuple-element.159), channel_id=1, source_target_pairs={{0,1},{1,0},{2,3},{3,2},{4,5},{5,4},{6,7},{7,6},{8,9},{9,8},{10,11... | collective-permute-start | bytes 3538952 | tf_op jit(solution)/shard_map/ppermute | solution.py:287
  131.1 31.2 %collective-permute-start.18 = (bf16[1076,1152]{1,0:T(8,128)(2,1)}, bf16[1076,1152]{1,0:T(8,128)(2,1)}, u32[]{:S(2)}, u32[]{:S(2)}) collective-permute-start(bf16[1076,1152]{1,0:T(8,128)(2,1)} %w2_ref.3), channel_id=1, source_target_pairs={{0,1},{1,0},{2,3},{3,2},{4,5},{5,4},{6,7},{7,6},{8,9},{9,8},{10,11... | collective-permute-start | bytes 7437320 | tf_op jit(solution)/shard_map/ppermute | solution.py:287
  152.2 56.3 %collective-permute-start.12 = (bf16[1076,1152]{1,0:T(8,128)(2,1)}, bf16[1076,1152]{1,0:T(8,128)(2,1)}, u32[]{:S(2)}, u32[]{:S(2)}) collective-permute-start(bf16[1076,1152]{1,0:T(8,128)(2,1)} %bitcast.168), channel_id=1, source_target_pairs={{0,2},{1,3},{2,0},{3,1},{4,6},{5,7},{6,4},{7,5},{8,10},{9,11},{10,... | collective-permute-start | bytes 7437320 | tf_op jit(solution)/shard_map/ppermute | solution.py:287
  155.3 38.8 %collective-permute-start.13 = (bf16[1024,1152]{1,0:T(8,128)(2,1)}, bf16[1024,1152]{1,0:T(8,128)(2,1)}, u32[]{:S(2)}, u32[]{:S(2)}) collective-permute-start(bf16[1024,1152]{1,0:T(8,128)(2,1)} %fusion.14.h_ref), channel_id=1, source_target_pairs={{0,1},{1,0},{2,3},{3,2},{4,5},{5,4},{6,7},{7,6},{8,9},{9,8},{10,11... | collective-permute-start | bytes 7077896 | tf_op jit(solution)/shard_map/ppermute | solution.py:287
  208.4 57.2 %collective-permute-start.20 = (bf16[1076,1152]{1,0:T(8,128)(2,1)}, bf16[1076,1152]{1,0:T(8,128)(2,1)}, u32[]{:S(2)}, u32[]{:S(2)}) collective-permute-start(bf16[1076,1152]{1,0:T(8,128)(2,1)} %w2_ref.3), channel_id=1, source_target_pairs={{0,2},{1,3},{2,0},{3,1},{4,6},{5,7},{6,4},{7,5},{8,10},{9,11},{10,... | collective-permute-start | bytes 7437320 | tf_op jit(solution)/shard_map/ppermute | solution.py:287
  208.9 123.9 %collective-permute-start.41 = (bf16[2,256,1152]{2,1,0:T(8,128)(2,1)}, bf16[2,256,1152]{2,1,0:T(8,128)(2,1)}, u32[]{:S(2)}, u32[]{:S(2)}) collective-permute-start(bf16[2,256,1152]{2,1,0:T(8,128)(2,1)} %get-tuple-element.159), channel_id=1, source_target_pairs={{0,2},{1,3},{2,0},{3,1},{4,6},{5,7},{6,4},{7,5},{8,10},{9,11},{10,... | collective-permute-start | bytes 3538952 | tf_op jit(solution)/shard_map/ppermute | solution.py:287
  219.4 217.7 %collective-permute-start.39 = (bf16[1024,1152]{1,0:T(8,128)(2,1)}, bf16[1024,1152]{1,0:T(8,128)(2,1)}, u32[]{:S(2)}, u32[]{:S(2)}) collective-permute-start(bf16[1024,1152]{1,0:T(8,128)(2,1)} %fusion.14.h_ref), channel_id=1, source_target_pairs={{0,2},{1,3},{2,0},{3,1},{4,6},{5,7},{6,4},{7,5},{8,10},{9,11},{10,... | collective-permute-start | bytes 7077896 | tf_op jit(solution)/shard_map/ppermute | solution.py:287
  445.4 31.9 %collective-permute-start.22 = (bf16[256,1152]{1,0:T(8,128)(2,1)}, bf16[256,1152]{1,0:T(8,128)(2,1)S(1)}, u32[]{:S(2)}, u32[]{:S(2)}) collective-permute-start(bf16[256,1152]{1,0:T(8,128)(2,1)} %get-tuple-element.156), channel_id=1, source_target_pairs={{0,1},{1,0},{2,3},{3,2},{4,5},{5,4},{6,7},{7,6},{8,9},{9,8},{10,11... | collective-permute-start | bytes 1769480 | tf_op jit(solution)/shard_map/ppermute | solution.py:287
  445.4 33.2 %collective-permute-start.23 = (bf16[256,1152]{1,0:T(8,128)(2,1)}, bf16[256,1152]{1,0:T(8,128)(2,1)S(1)}, u32[]{:S(2)}, u32[]{:S(2)}) collective-permute-start(bf16[256,1152]{1,0:T(8,128)(2,1)} %get-tuple-element.155), channel_id=1, source_target_pairs={{0,2},{1,3},{2,0},{3,1},{4,6},{5,7},{6,4},{7,5},{8,10},{9,11},{10,... | collective-permute-start | bytes 1769480 | tf_op jit(solution)/shard_map/ppermute | solution.py:287
  447.0 32.2 %collective-permute-start.24 = (bf16[256,1152]{1,0:T(8,128)(2,1)}, bf16[256,1152]{1,0:T(8,128)(2,1)S(1)}, u32[]{:S(2)}, u32[]{:S(2)}) collective-permute-start(bf16[256,1152]{1,0:T(8,128)(2,1)} %get-tuple-element.154), channel_id=1, source_target_pairs={{0,3},{1,2},{2,1},{3,0},{4,7},{5,6},{6,5},{7,4},{8,11},{9,10},{10,... | collective-permute-start | bytes 1769480 | tf_op jit(solution)/shard_map/ppermute | solution.py:287
  447.3 32.2 %collective-permute-start.25 = (bf16[256,1152]{1,0:T(8,128)(2,1)}, bf16[256,1152]{1,0:T(8,128)(2,1)S(1)}, u32[]{:S(2)}, u32[]{:S(2)}) collective-permute-start(bf16[256,1152]{1,0:T(8,128)(2,1)} %get-tuple-element.148), channel_id=1, source_target_pairs={{0,1},{1,0},{2,3},{3,2},{4,5},{5,4},{6,7},{7,6},{8,9},{9,8},{10,11... | collective-permute-start | bytes 1769480 | tf_op jit(solution)/shard_map/ppermute | solution.py:287
  478.6 29.4 %collective-permute-start.43 = (bf16[2,256,1152]{2,1,0:T(8,128)(2,1)}, bf16[2,256,1152]{2,1,0:T(8,128)(2,1)S(1)}, u32[]{:S(2)}, u32[]{:S(2)}) collective-permute-start(bf16[2,256,1152]{2,1,0:T(8,128)(2,1)} %copy-done.17), channel_id=1, source_target_pairs={{0,1},{1,0},{2,3},{3,2},{4,5},{5,4},{6,7},{7,6},{8,9},{9,8},{10,11... | collective-permute-start | bytes 3538952 | tf_op jit(solution)/shard_map/ppermute | solution.py:287
  479.6 34.3 %collective-permute-start.40 = (bf16[1024,1152]{1,0:T(8,128)(2,1)}, bf16[1024,1152]{1,0:T(8,128)(2,1)S(1)}, u32[]{:S(2)}, u32[]{:S(2)}) collective-permute-start(bf16[1024,1152]{1,0:T(8,128)(2,1)} %collective-permute-done.39), channel_id=1, source_target_pairs={{0,1},{1,0},{2,3},{3,2},{4,5},{5,4},{6,7},{7,6},{8,9},{9,8},{10,11... | collective-permute-start | bytes 7077896 | tf_op jit(solution)/shard_map/ppermute | solution.py:287
  501.5 34.7 %collective-permute-start.31 = (f32[3,288,1152]{2,1,0:T(8,128)}, f32[3,288,1152]{2,1,0:T(8,128)}, u32[]{:S(2)}, u32[]{:S(2)}) collective-permute-start(f32[3,288,1152]{2,1,0:T(8,128)} %get-tuple-element.114), channel_id=1, source_target_pairs={{0,1},{1,0},{2,3},{3,2},{4,5},{5,4},{6,7},{7,6},{8,9},{9,8},{10,11... | collective-permute-start | bytes 11943944 | tf_op jit(solution)/shard_map/ppermute | solution.py:287
  506.5 57.0 %collective-permute-start.36 = (f32[288,1152]{1,0:T(8,128)S(1)}, f32[288,1152]{1,0:T(8,128)S(1)}, u32[]{:S(2)}, u32[]{:S(2)}) collective-permute-start(f32[288,1152]{1,0:T(8,128)S(1)} %copy-done.46), channel_id=1, source_target_pairs={{0,1},{1,0},{2,3},{3,2},{4,5},{5,4},{6,7},{7,6},{8,9},{9,8},{10,11... | collective-permute-start | bytes 3981320 | tf_op jit(solution)/shard_map/ppermute | solution.py:287
  508.0 58.8 %collective-permute-start.30 = (f32[3,288,1152]{2,1,0:T(8,128)}, f32[3,288,1152]{2,1,0:T(8,128)}, u32[]{:S(2)}, u32[]{:S(2)}) collective-permute-start(f32[3,288,1152]{2,1,0:T(8,128)} %get-tuple-element.112), channel_id=1, source_target_pairs={{0,1},{1,0},{2,3},{3,2},{4,5},{5,4},{6,7},{7,6},{8,9},{9,8},{10,11... | collective-permute-start | bytes 11943944 | tf_op jit(solution)/shard_map/ppermute | solution.py:287
  512.3 51.3 %collective-permute-start.38 = (f32[288,1152]{1,0:T(8,128)}, f32[288,1152]{1,0:T(8,128)}, u32[]{:S(2)}, u32[]{:S(2)}) collective-permute-start(f32[288,1152]{1,0:T(8,128)} %convolution_add_fusion.4), channel_id=1, source_target_pairs={{0,2},{1,3},{2,0},{3,1},{4,6},{5,7},{6,4},{7,5},{8,10},{9,11},{10,... | collective-permute-start | bytes 3981320 | tf_op jit(solution)/shard_map/ppermute | solution.py:287
  540.1 89.2 %collective-permute-start.32 = (f32[3,288,1152]{2,1,0:T(8,128)S(1)}, f32[3,288,1152]{2,1,0:T(8,128)S(1)}, u32[]{:S(2)}, u32[]{:S(2)}) collective-permute-start(f32[3,288,1152]{2,1,0:T(8,128)S(1)} %add.176), channel_id=1, source_target_pairs={{0,2},{1,3},{2,0},{3,1},{4,6},{5,7},{6,4},{7,5},{8,10},{9,11},{10,... | collective-permute-start | bytes 11943944 | tf_op jit(solution)/shard_map/ppermute | solution.py:287
  (85 other events, 960.8 us)

commit v3 on v2

--- a/solution.py
+++ b/solution.py
@@ -11,11 +11,19 @@
 PAIR = 2 * HEAD
 FWD_QUERIES = 1024
 BWD_QUERIES = 512
-ROWS = 512
+ROWS = 256
 GELU_C = math.sqrt(2.0 / math.pi)
 F32 = jnp.float32
 BF16 = jnp.bfloat16
 LOG2E = 1.4426950408889634
+
+
+def by_row(i, *_):
+    return i, 0
+
+
+def stay(*_):
+    return 0, 0
 
 
 def layer_norm(rows, ln_gain, ln_bias):
@@ -113,8 +121,8 @@
     return pl.pallas_call(
         attn_fwd_kernel,
         grid=(pairs,),
-        in_specs=[trio(width), trio(1), pl.BlockSpec((width, tokens), lambda i: (0, 0), pipeline_mode=pl.Buffered(1))],
-        out_specs=[trio(tokens), pl.BlockSpec((PAIR, tokens), lambda i: (i, 0)),
+        in_specs=[trio(width), trio(1), pl.BlockSpec((width, tokens), stay, pipeline_mode=pl.Buffered(1))],
+        out_specs=[trio(tokens), pl.BlockSpec((PAIR, tokens), by_row),
                    pl.BlockSpec((1, 8, tokens), lambda i: (i, 0, 0))],
         out_shape=[jax.ShapeDtypeStruct((3, rows, tokens), BF16), jax.ShapeDtypeStruct((rows, tokens), BF16),
                    jax.ShapeDtypeStruct((pairs, 8, tokens), F32)],
@@ -132,8 +140,8 @@
     return pl.pallas_call(
         attn_bwd_kernel,
         grid=(pairs,),
-        in_specs=[trio(tokens), pl.BlockSpec((PAIR, tokens), lambda i: (i, 0)), pl.BlockSpec((1, 8, tokens), lambda i: (i, 0, 0)),
-                  pl.BlockSpec((tokens, width), lambda i: (0, 0), pipeline_mode=pl.Buffered(1))],
+        in_specs=[trio(tokens), pl.BlockSpec((PAIR, tokens), by_row), pl.BlockSpec((1, 8, tokens), lambda i: (i, 0, 0)),
+                  pl.BlockSpec((tokens, width), stay, pipeline_mode=pl.Buffered(1))],
         out_specs=[trio(tokens), trio(width), pl.BlockSpec((3, 1, 8, PAIR), lambda i: (0, i, 0, 0))],
         out_shape=[jax.ShapeDtypeStruct((3, rows, tokens), BF16), jax.ShapeDtypeStruct((3, rows, width), F32),
                    jax.ShapeDtypeStruct((3, pairs, 8, PAIR), F32)],
@@ -187,7 +195,7 @@
     dh_ref[...] = d_h + d_h_b
 
 
-def norm_bwd_tile(x_ref, d_h, res_ref, gain_ref, out_ref, dgain_ref, dbias_ref, dout_ref):
+def norm_bwd_tile(x_ref, d_h, res_ref, gain_ref, out_refs, dgain_ref, dbias_ref, dout_ref):
     x = x_ref[...].astype(F32)
     centered = x - jnp.mean(x, axis=-1, keepdims=True)
     inv = lax.rsqrt(jnp.mean(centered * centered, axis=-1, keepdims=True) + LN_EPS)
@@ -198,10 +206,20 @@
     tilt = jnp.mean(d_unit * unit, axis=-1, keepdims=True)
     d_x = inv * (d_unit - jnp.mean(d_unit, axis=-1, keepdims=True) - unit * tilt)
     out = (res_ref[...].astype(F32) + d_x).astype(BF16)
-    out_ref[...] = out
+    store_slab(out_refs, out)
     add_row_sum(dgain_ref, d_h * unit)
     if dout_ref is not None:
         add_row_sum(dout_ref, out)
+
+
+def store_slab(refs, rows):
+    if len(refs) == 1:
+        refs[0][...] = rows
+        return
+    for k, ref in enumerate(refs):
+        @pl.when(pl.program_id(0) == k)
+        def _(ref=ref):
+            ref[...] = rows
 
 
 def norm_one_kernel(*refs):
@@ -209,34 +227,34 @@
     d_h = dot_tn(d_refs[0][...], w_refs[0][...])
     for d_ref, w_ref in zip(d_refs[1:], w_refs[1:]):
         d_h += dot_tn(d_ref[...], w_ref[...])
-    gain_ref, out_ref, dgain_ref, dbias_ref = rest
-    norm_bwd_tile(x_ref, d_h.astype(BF16), res_ref, gain_ref, out_ref, dgain_ref, dbias_ref, None)
+    gain_ref, outs, (dgain_ref, dbias_ref) = rest[0], rest[1:5], rest[5:]
+    norm_bwd_tile(x_ref, d_h.astype(BF16), res_ref, gain_ref, outs, dgain_ref, dbias_ref, None)
 
 
 def norm_one_bwd(d_qkv, w_qkv, x, residual, gain):
     tokens, width = x.shape
-    tile = 256
-    rows = pl.BlockSpec((tile, width), lambda i: (i, 0))
-    whole = lambda op: pl.BlockSpec(op.shape, lambda i: (0, 0), pipeline_mode=pl.Buffered(1))
+    tile = tokens // 4
+    rows = pl.BlockSpec((tile, width), by_row)
+    whole = lambda op: pl.BlockSpec(op.shape, stay, pipeline_mode=pl.Buffered(1))
     depth = d_qkv[0].shape[0]
     return pl.pallas_call(
         norm_one_kernel,
         grid=(tokens // tile,),
         in_specs=[pl.BlockSpec((depth, tile), lambda i: (0, i))] * 4 + [rows, rows] + [whole(w) for w in w_qkv] + [whole(gain)],
-        out_specs=[rows] + [pl.BlockSpec((1, width), lambda i: (0, 0))] * 2,
-        out_shape=[jax.ShapeDtypeStruct((tokens, width), BF16)] + [jax.ShapeDtypeStruct((1, width), F32)] * 2,
+        out_specs=[pl.BlockSpec((tile, width), stay)] * 4 + [pl.BlockSpec((1, width), stay)] * 2,
+        out_shape=[jax.ShapeDtypeStruct((tile, width), BF16)] * 4 + [jax.ShapeDtypeStruct((1, width), F32)] * 2,
         cost_estimate=pl.CostEstimate(flops=8 * depth * tokens * width, bytes_accessed=30 * depth * tokens, transcendentals=0),
         name="nob",
     )(*d_qkv, x, residual, *w_qkv, gain)
 
 
 def mlp_far_kernel(ua_ref, ub_ref, d_ref, w1a_ref, w1b_ref, w2a_ref, w2b_ref, x_ref, b_ref, gain_ref, yp_ref, dhp_ref,
-                   y_ref, out_ref, dgain_ref, dbias_ref, dout_ref):
+                   out_ref, dgain_ref, dbias_ref, dout_ref, *y_refs):
     _, _, y, d_h = mlp_block(ua_ref, d_ref, w1a_ref, w2a_ref)
     _, _, y_b, d_h_b = mlp_block(ub_ref, d_ref, w1b_ref, w2b_ref)
-    y_ref[...] = (x_ref[...].astype(F32) + (yp_ref[...] + (y + y_b)) + b_ref[...]).astype(BF16)
+    store_slab(y_refs, (x_ref[...].astype(F32) + (yp_ref[...] + (y + y_b)) + b_ref[...]).astype(BF16))
     d_h = (dhp_ref[...] + (d_h + d_h_b)).astype(BF16)
-    norm_bwd_tile(x_ref, d_h, d_ref, gain_ref, out_ref, dgain_ref, dbias_ref, dout_ref)
+    norm_bwd_tile(x_ref, d_h, d_ref, gain_ref, (out_ref,), dgain_ref, dbias_ref, dout_ref)
 
 
 def mlp_own_kernel(h_ref, d_ref, w1_ref, w2_ref, b_ref, g_ref, du_ref, dus_ref):
@@ -249,13 +267,95 @@
     add_row_sum(dus_ref, d_u)
 
 
-def row_call(kernel, tiled, fixed, outs, flops, order=None, sums=(), tile=ROWS):
+def gather_rows_kernel(core_ref, a_ref, b_ref, c_ref, d_ref, out_ref):
+    refs = (a_ref, b_ref, c_ref, d_ref)
+    for step in range(8):
+        @pl.when(pl.program_id(0) == step)
+        def _(step=step):
+            out_ref[...] = refs[(step % 4) ^ (step // 4)][0]
+
+
+def gather_rows(core, slabs, images=2):
+    _, tokens, width = slabs[0].shape
+    pick = lambda i, core: (lax.rem(core[0] + lax.div(i, 4), 2), 0, 0)
+    return pl.pallas_call(
+        gather_rows_kernel,
+        grid_spec=pltpu.PrefetchScalarGridSpec(
+            num_scalar_prefetch=1, grid=(4 * images,),
+            in_specs=[pl.BlockSpec((1, tokens, width), pick)] * 4,
+            out_specs=pl.BlockSpec((tokens, width), by_row)),
+        out_shape=jax.ShapeDtypeStruct((4 * images * tokens, width), slabs[0].dtype),
+        cost_estimate=pl.CostEstimate(flops=30 * 8 * tokens * width, bytes_accessed=32 * tokens * width, transcendentals=0),
+        name="gr",
+    )(core[None], *slabs)
+
+
+def mlp_own_far_kernel(core_ref, ha_ref, hb_ref, da_ref, db_ref, dc_ref, dd_ref, w1_ref, w2_ref, b_ref,
+                       g_ref, du_ref, h_ref, d_ref, dus_ref):
+    gather_rows_kernel(core_ref, da_ref, db_ref, dc_ref, dd_ref, d_ref)
+
+    @pl.when(pl.program_id(0) < 4)
+    def _():
+        h_ref[...] = ha_ref[...]
+
+    @pl.when(pl.program_id(0) >= 4)
+    def _():
+        h_ref[...] = hb_ref[...]
+
+    mlp_own_kernel(h_ref, d_ref, w1_ref, w2_ref, b_ref, g_ref, du_ref, dus_ref)
+
+
+def mlp_own_far(core, h_two, h_diag, slabs, w_1, w_2, b_1):
+    _, tokens, width = slabs[0].shape
+    cols = w_1.shape[0]
+    pick = lambda i, core: (lax.rem(core[0] + lax.div(i, 4), 2), 0, 0)
+    fixed = lambda op: pl.BlockSpec(op.shape, stay, pipeline_mode=pl.Buffered(1))
+    tile = lambda c: pl.BlockSpec((tokens, c), by_row)
+    return pl.pallas_call(
+        mlp_own_far_kernel,
+        grid_spec=pltpu.PrefetchScalarGridSpec(
+            num_scalar_prefetch=1, grid=(8,),
+            in_specs=[pl.BlockSpec((tokens, width), lambda i, core: (jnp.minimum(i, 3), 0)),
+                      pl.BlockSpec((tokens, width), lambda i, core: (jnp.maximum(i - 4, 0), 0))]
+            + [pl.BlockSpec((1, tokens, width), pick)] * 4 + [fixed(w_1), fixed(w_2), fixed(b_1)],
+            out_specs=[tile(cols), tile(cols), tile(width), tile(width), pl.BlockSpec((1, cols), stay)]),
+        out_shape=[jax.ShapeDtypeStruct((8 * tokens, c), BF16) for c in (cols, cols, width, width)]
+        + [jax.ShapeDtypeStruct((1, cols), F32)],
+        cost_estimate=pl.CostEstimate(flops=32 * tokens * width * cols, bytes_accessed=64 * tokens * width, transcendentals=0),
+        name="mof",
+    )(core[None], h_two, h_diag, *slabs, w_1, w_2, b_1)
+
+
+def order_kernel(me_ref, a_ref, b_ref, c_ref, d_ref, out_ref):
+    refs = (a_ref, b_ref, c_ref, d_ref)
+    for step in range(4):
+        @pl.when(pl.program_id(0) == step)
+        def _(step=step):
+            out_ref[0] = refs[step][...]
+
+
+def order_parts(me, parts):
+    tokens, width = parts[0].shape
+    return pl.pallas_call(
+        order_kernel,
+        grid_spec=pltpu.PrefetchScalarGridSpec(
+            num_scalar_prefetch=1, grid=(4,),
+            in_specs=[pl.BlockSpec((tokens, width), stay)] * 4,
+            out_specs=pl.BlockSpec((1, tokens, width), lambda i, me: (me[0] ^ i, 0, 0))),
+        out_shape=jax.ShapeDtypeStruct((4, tokens, width), parts[0].dtype),
+        cost_estimate=pl.CostEstimate(flops=30 * 4 * tokens * width, bytes_accessed=16 * tokens * width, transcendentals=0),
+        name="op",
+    )(me[None], *parts)
+
+
+def row_call(kernel, tiled, fixed, outs, flops, order=None, sums=(), slabs=0):
+    tile = ROWS
     rows = tiled[0].shape[0]
     operands = tiled + fixed if order is None else [(tiled + fixed)[i] for i in order]
     is_tiled = [True] * len(tiled) + [False] * len(fixed)
     is_tiled = is_tiled if order is None else [is_tiled[i] for i in order]
-    in_specs = [pl.BlockSpec((tile, op.shape[1]), lambda i: (i, 0)) if t
-                else pl.BlockSpec(op.shape, lambda i: (0, 0), pipeline_mode=pl.Buffered(1))
+    in_specs = [pl.BlockSpec((tile, op.shape[1]), by_row) if t
+                else pl.BlockSpec(op.shape, stay, pipeline_mode=pl.Buffered(1))
                 for op, t in zip(operands, is_tiled)]
     size = sum(op.size * op.dtype.itemsize for op in operands) + sum(rows * c * d.dtype.itemsize for c, d in
                                                                      [(c, jnp.zeros((), d)) for c, d in outs])
@@ -263,8 +363,10 @@
         kernel,
         grid=(rows // tile,),
         in_specs=in_specs,
-        out_specs=[pl.BlockSpec((tile, c), lambda i: (i, 0)) for c, _ in outs] + [pl.BlockSpec((1, c), lambda i: (0, 0)) for c in sums],
-        out_shape=[jax.ShapeDtypeStruct((rows, c), d) for c, d in outs] + [jax.ShapeDtypeStruct((1, c), F32) for c in sums],
+        out_specs=[pl.BlockSpec((tile, c), by_row) for c, _ in outs] + [pl.BlockSpec((1, c), stay) for c in sums]
+        + [pl.BlockSpec((tile, slabs), stay)] * (4 if slabs else 0),
+        out_shape=[jax.ShapeDtypeStruct((rows, c), d) for c, d in outs] + [jax.ShapeDtypeStruct((1, c), F32) for c in sums]
+        + [jax.ShapeDtypeStruct((tile, slabs), BF16)] * (4 if slabs else 0),
         cost_estimate=pl.CostEstimate(flops=flops, bytes_accessed=size, transcendentals=0),
     )(*operands)
 
@@ -297,7 +399,6 @@
     def layer_step(x, d_out, ln1_gain, ln1_bias, w_q, b_q, w_k, w_v, b_v, w_o, b_o, ln2_gain, ln2_bias, w_1, b_1, w_2, b_2):
         me = lax.axis_index('tp')
         width = x.shape[2]
-        slab = x.shape[1]
         local_rows = w_o.shape[0] * w_o.shape[1]
 
         def image(shard, k):
@@ -306,10 +407,9 @@
         def to_image(shard):
             return jnp.concatenate([image(shard, 0)] + [swap(image(shard, k), k) for k in (1, 2, 3)], axis=0)
 
-        def to_tokens(rows):
-            parts = [rows[:slab]] + [swap(rows[k * slab:(k + 1) * slab], k) for k in (1, 2, 3)]
-            stacked = jnp.stack(parts)
-            return jnp.stack([lax.dynamic_index_in_dim(stacked, me ^ i, 0, keepdims=False) for i in range(4)])
+        def to_tokens(slabs):
+            parts = [slabs[0]] + [swap(slabs[k], k) for k in (1, 2, 3)]
+            return order_parts(me, parts)
 
         x_img = to_image(x)
         w_qkv_own = jnp.stack([w.reshape(width, local_rows).T for w in (w_q, w_k, w_v)])
@@ -330,9 +430,6 @@
         w_two_sent = send(w_2)
         d_there_near, d_there_two = swap(d_there, 1), swap(d_here, 2)
 
-        def rows_of(pairs, which):
-            return jnp.concatenate([lax.dynamic_index_in_dim(p, which, 0, keepdims=False) for p in pairs], axis=0)
-
         x_f32 = x_img.astype(F32)
         h_one = layer_norm(x_f32, ln1_gain, ln1_bias).astype(BF16)
         h_one_t = lax.optimization_barrier(h_one.T)
@@ -349,7 +446,7 @@
         attn_out = dot_tn(jnp.concatenate(mixed, axis=0), jnp.concatenate(w_out, axis=0))
         x_mid = (x_f32 + attn_out + b_o).astype(BF16)
         mid_f32 = x_mid.astype(F32)
-        h_two = layer_norm(mid_f32, ln2_gain, ln2_bias).astype(BF16)
+        h_two = lax.optimization_barrier(layer_norm(mid_f32, ln2_gain, ln2_bias).astype(BF16))
         h_sent = send(h_two)
 
         cols = w_1.shape[1]
@@ -368,8 +465,8 @@
 
         d_here_two, _ = lax.optimization_barrier((d_here_two, pre_near[1]))
         d_here_diag = swap(d_here_two, 1)
-        d_img = rows_of((d_here, d_here_near, d_here_two, d_here_diag), core)
-        d_sib = rows_of((d_here_near, d_here, d_here_diag, d_here_two), 1 - core)
+        d_img = gather_rows(core, (d_here, d_here_near, d_here_two, d_here_diag), 1)
+        d_sib = gather_rows(1 - core, (d_here_near, d_here, d_here_diag, d_here_two), 1)
         g_own, d_u_own, y_part, d_h_part, d_u_sum, d_sum = row_call(
             mlp_near_kernel, [*pre_near, d_img], [*w_one_sent[:2], *w_two_sent[:2]],
             [(cols, BF16)] * 2 + [(width, F32)] * 2, 6 * mm, sums=(cols, width))
@@ -381,11 +478,11 @@
         g_w_2 = sum(dot_tn(p[2], p[1]) for p in parts)
         g_w_1, g_w_2 = lax.optimization_barrier((g_w_1, g_w_2))
         w_two = land(w_two_sent, pre_far[1])
-        y_img, d_mid, g_ln2_gain, g_ln2_bias, d_mid_sum = row_call(
+        d_mid, g_ln2_gain, g_ln2_bias, d_mid_sum, *y_slabs = row_call(
             mlp_far_kernel, [*pre_far, d_img, x_mid, y_part, d_h_part],
-            [*w_one[2:], *w_two[2:], b_2.astype(F32)[None, :], ln2_gain[None, :]], [(width, BF16)] * 2, 6 * mm,
-            order=(0, 1, 2, 6, 7, 8, 9, 3, 10, 11, 4, 5), sums=(width,) * 3)
-        y_out = to_tokens(y_img)
+            [*w_one[2:], *w_two[2:], b_2.astype(F32)[None, :], ln2_gain[None, :]], [(width, BF16)], 6 * mm,
+            order=(0, 1, 2, 6, 7, 8, 9, 3, 10, 11, 4, 5), sums=(width,) * 3, slabs=width)
+        y_out = to_tokens(y_slabs)
 
         def reduce_cross(part):
             return swap(part[2] + swap(part[3], 1), 2)
@@ -402,18 +499,17 @@
         g_w_qkv = reduce_near(g_qkv_part, reduce_cross(g_qkv_part)).astype(BF16)
         g_w_q, g_w_k, g_w_v = [g_w_qkv[i].T.reshape(w_q.shape) for i in range(3)]
 
-        grad_x_img, g_ln1_gain, g_ln1_bias = norm_one_bwd(
+        *grad_x_slabs, g_ln1_gain, g_ln1_bias = norm_one_bwd(
             [d.reshape(-1, d.shape[2]) for d in d_qkv], [w.reshape(-1, width) for w in w_qkv], x_img, d_mid, ln1_gain[None, :])
-        h_all = land(h_sent, grad_x_img)
+        h_all = land(h_sent, grad_x_slabs[3])
         d_there_two, _ = lax.optimization_barrier((d_there_two, d_mid))
         d_there_diag = swap(d_there_two, 1)
-        d_far = jnp.concatenate([rows_of((d_there_two, d_there_diag, d_there, d_there_near), core),
-                                 rows_of((d_there_diag, d_there_two, d_there_near, d_there), 1 - core)], axis=0)
-        part_far = own_columns(jnp.concatenate(h_all[2:], axis=0), d_far)
-        g_w_1 = (g_w_1 + dot_tn(part_far[3], part_far[0])).astype(BF16).T
-        g_w_2 = (g_w_2 + dot_tn(part_far[2], part_far[1])).astype(BF16)
-        g_b_1 = (parts[0][4] + parts[1][4] + part_far[4])[0].astype(BF16)
-        grad_x = to_tokens(grad_x_img)
+        g_far, d_u_far, h_far, d_far, d_u_far_sum = mlp_own_far(
+            core, h_all[2], h_all[3], (d_there_two, d_there_diag, d_there, d_there_near), w_one_own, w_2, b_one[0])
+        g_w_1 = (g_w_1 + dot_tn(d_u_far, h_far)).astype(BF16).T
+        g_w_2 = (g_w_2 + dot_tn(g_far, d_far)).astype(BF16)
+        g_b_1 = (parts[0][4] + parts[1][4] + d_u_far_sum)[0].astype(BF16)
+        grad_x = to_tokens(grad_x_slabs)
 
         b_part = [b[:, :, 0] for b in b_part]
         g_b_qkv = reduce_near(b_part, reduce_cross(b_part)).astype(BF16)

time: 642 us -> 657 us (1.023)
  waiting for transfers between devices: 181 us -> 212 us
  local copies, waits for them, and re-layouts: 57.6 us -> 32.8 us
  Pallas kernels: 265 us -> 286 us
  other arithmetic: 33.4 us -> 23.6 us
    pallas_call x0 -> x5, Pallas kernels: none -> 37.7 us  [the longest x1 23.4 us: mlp_own_far(): pl.pallas_call(mlp_own_far_kernel, grid_spec=pltpu.PrefetchScalarGridSpec...]
    ppermute x44, waiting for transfers between devices: 181 us -> 212 us  [swap(): return lax.ppermute(value, 'tp', [(i, i ^ k) for i in range(4)])]
    pallas_call x6 -> x5, Pallas kernels: 121 us -> 103 us  [row_call(): pl.pallas_call(kernel, grid=(rows // tile,), in_specs=in_specs, out_specs...]
    unnamed x139 -> x117, local copies, waits for them, and re-layouts: 10.4 us -> 1.41 us
  transfers between devices with their start and end apart: 44 -> 44, of which waited for: 11 -> 12; matrix products, arithmetic and copies ran while one was open for 23% -> 19% of each run, Pallas kernels for 42% -> 44%
where the time goes in v3:
time: 657 us; the launch traced here: 653 us
  Pallas kernels  286 us (44%)
  waiting for transfers between devices  212 us (32%)
  matrix products  73.3 us (11%)
  local copies, waits for them, and re-layouts  32.8 us (5%)
  starting transfers between devices  23.6 us (4%)
  other arithmetic  23.6 us (4%)
    ppermute x44, waiting for transfers between devices, swap(): return lax.ppermute(value, 'tp', [(i, i ^ k) for i in range(4)])  212 us
    pallas_call x5, Pallas kernels, row_call(): pl.pallas_call(kernel, grid=(rows // tile,), in_specs=in_specs, out_specs...  103 us
    pallas_call x4, Pallas kernels, attn_bwd(): pl.pallas_call(attn_bwd_kernel, grid=(pairs,), in_specs=[trio(tokens), pl...  73.4 us
    pallas_call x4, Pallas kernels, attn_fwd(): pl.pallas_call(attn_fwd_kernel, grid=(pairs,), in_specs=[trio(width), tri...  49.7 us
    dot_general x7, matrix products, dot_tn(): lax.dot_general(a, b, (((0,), (0,)), ((), ())), preferred_element_type=F32)  48.7 us
    ppermute x44, starting transfers between devices, swap(): return lax.ppermute(value, 'tp', [(i, i ^ k) for i in range(4)])  23.6 us
    pallas_call x1, Pallas kernels, mlp_own_far(): pl.pallas_call(mlp_own_far_kernel, grid_spec=pltpu.PrefetchScalarGridSpec...  23.4 us
    pallas_call x1, Pallas kernels, norm_one_bwd(): pl.pallas_call(norm_one_kernel, grid=(tokens // tile,), in_specs=[pl.Bloc...  22 us
  transfers between devices with their start and end apart: 44, of which 12 were waited for; matrix products, arithmetic and copies ran while one was open for 19% of the time, Pallas kernels for 44%

profile of v3, /device:TPU:0, one launch (start us, length us, event | category | flops | bytes accessed | tf_op | source)
XLA Modules:
  0.0 652.5 jit_solution(17892039107044781742)
XLA Ops:
  18.5 49.6 %collective-permute-done.2 = bf16[256,1152]{1,0:T(8,128)(2,1)S(1)} collective-permute-done((bf16[256,1152]{1,0:T(8,128)(2,1)}, bf16[256,1152]{1,0:T(8,128)(2,1)S(1)}, u32[]{:S(2)}, u32[]{:S(2)}) %collective-permute-start.2) | collective-permute-done | bytes 589856 | tf_op jit(solution)/shard_map/ppermute | solution.py:389
  68.1 13.1 %collective-permute-done.1 = bf16[256,1152]{1,0:T(8,128)(2,1)S(1)} collective-permute-done((bf16[256,1152]{1,0:T(8,128)(2,1)S(1)}, bf16[256,1152]{1,0:T(8,128)(2,1)S(1)}, u32[]{:S(2)}, u32[]{:S(2)}) %collective-permute-start.1) | collective-permute-done | bytes 589856 | tf_op jit(solution)/shard_map/ppermute | solution.py:389
  91.5 12.3 %af.5 = (bf16[3,288,1024]{2,1,0:T(8,128)(2,1)}, bf16[288,1024]{1,0:T(8,128)(2,1)}, f32[2,8,1024]{2,1,0:T(8,128)}) custom-call(bf16[3,288,1152]{2,1,0:T(8,128)(2,1)} %collective-permute-done.3.w_ref, f32[3,288,1]{2,1,0:T(8,128)} %copy.76.b_ref, bf16[1152,1024]{1,0:T(8,128)(2,1)} %copy.75.h_ref), custom_call_target="tpu_custom_call" | custom-call | flops 6870269952 | bytes 4128768 | tf_op jit(solution)/shard_map/af/pallas_call | solution.py:121
  115.9 12.3 %af.6 = (bf16[3,288,1024]{2,1,0:T(8,128)(2,1)}, bf16[288,1024]{1,0:T(8,128)(2,1)}, f32[2,8,1024]{2,1,0:T(8,128)}) custom-call(bf16[3,288,1152]{2,1,0:T(8,128)(2,1)} %collective-permute-done.5.w_ref, f32[3,288,1]{2,1,0:T(8,128)} %copy.78.b_ref, bf16[1152,1024]{1,0:T(8,128)(2,1)} %copy.75.h_ref), custom_call_target="tpu_custom_call" | custom-call | flops 6870269952 | bytes 4128768 | tf_op jit(solution)/shard_map/af/pallas_call | solution.py:121
  128.7 12.5 %af.4 = (bf16[3,288,1024]{2,1,0:T(8,128)(2,1)}, bf16[288,1024]{1,0:T(8,128)(2,1)}, f32[2,8,1024]{2,1,0:T(8,128)}) custom-call(bf16[3,288,1152]{2,1,0:T(8,128)(2,1)} %pad_maximum_fusion.1.w_ref, f32[3,288,1]{2,1,0:T(8,128)} %copy.74.b_ref, bf16[1152,1024]{1,0:T(8,128)(2,1)} %copy.75.h_ref), custom_call_target="tpu_custom_call" | custom-call | flops 6870269952 | bytes 4128768 | tf_op jit(solution)/shard_map/af/pallas_call | solution.py:121
  141.3 12.5 %af.7 = (bf16[3,288,1024]{2,1,0:T(8,128)(2,1)}, bf16[288,1024]{1,0:T(8,128)(2,1)}, f32[2,8,1024]{2,1,0:T(8,128)}) custom-call(bf16[3,288,1152]{2,1,0:T(8,128)(2,1)} %collective-permute-done.7.w_ref, f32[3,288,1]{2,1,0:T(8,128)} %copy.80.b_ref, bf16[1152,1024]{1,0:T(8,128)(2,1)} %copy.75.h_ref), custom_call_target="tpu_custom_call" | custom-call | flops 6870269952 | bytes 4128768 | tf_op jit(solution)/shard_map/af/pallas_call | solution.py:121
  164.0 11.1 %shard_map.296 = (bf16[1024,1076]{1,0:T(8,128)(2,1)}, bf16[1024,1076]{1,0:T(8,128)(2,1)}) custom-call(bf16[1024,1152]{1,0:T(8,128)(2,1)} %fusion.14.h_ref, bf16[1076,1152]{1,0:T(8,128)(2,1)} %bitcast.122, bf16[1076,1152]{1,0:T(8,128)(2,1)} %collective-permute-done.16.wb_ref.w1b_ref, f32[1,1076]{1,0:T(1,128)} %broadcast_in_dim.61.ba_ref.b_ref, ...), custom_call_target="tpu_custom_call" | custom-call | flops 5077204992 | bytes 11733408 | tf_op jit(solution)/shard_map/pallas_call | solution.py:362
  185.5 31.9 %shard_map.298 = (bf16[1024,1076]{1,0:T(8,128)(2,1)}, bf16[1024,1076]{1,0:T(8,128)(2,1)}, f32[1024,1152]{1,0:T(8,128)}, f32[1024,1152]{1,0:T(8,128)}, f32[1,1076]{1,0:T(1,128)}, /*index=5*/f32[1,1152]{1,0:T(1,128)}) custom-call(bf16[1024,1076]{1,0:T(8,128)(2,1)} %get-tuple-element.91.ua_ref, bf16[1024,1076]{1,0:T(8,128)(2,1)} %get-tuple-element.88.ub_ref, ...), custom_call_target="tpu_custom_call" | custom-call | flops 15231614976 | bytes 30527488 | tf_op jit(solution)/shard_map/pallas_call | solution.py:362
  217.5 12.2 %shard_map.297 = (bf16[1024,1076]{1,0:T(8,128)(2,1)}, bf16[1024,1076]{1,0:T(8,128)(2,1)}, f32[1,1076]{1,0:T(1,128)}) custom-call(bf16[1024,1152]{1,0:T(8,128)(2,1)} %collective-permute-done.13.h_ref, bf16[1024,1152]{1,0:T(8,128)(2,1)} %gr.2.d_ref, bf16[1076,1152]{1,0:T(8,128)(2,1)} %bitcast.125, bf16[1076,1152]{1,0:T(8,128)(2,1)} %w2_ref.3, ...), custom_call_target="tpu_custom_call" | custom-call | flops 5077204992 | bytes 14088400 | tf_op jit(solution)/shard_map/pallas_call | solution.py:362
  237.0 11.3 %shard_map.299 = (bf16[1024,1076]{1,0:T(8,128)(2,1)}, bf16[1024,1076]{1,0:T(8,128)(2,1)}) custom-call(bf16[1024,1152]{1,0:T(8,128)(2,1)} %fusion.14.h_ref, bf16[1076,1152]{1,0:T(8,128)(2,1)} %collective-permute-done.12.wa_ref.w1a_ref, bf16[1076,1152]{1,0:T(8,128)(2,1)} %collective-permute-done.19.wb_ref.w1b_ref, f32[1,1076]{1,0:T(1,128)} %broadcast_in_dim.64.ba_ref, ...), custom_call_target="tpu_custom_call" | custom-call | flops 5077204992 | bytes 11733408 | tf_op jit(solution)/shard_map/pallas_call | solution.py:362
  248.3 40.4 %collective-permute-done.20.w2a_ref = bf16[1076,1152]{1,0:T(8,128)(2,1)} collective-permute-done((bf16[1076,1152]{1,0:T(8,128)(2,1)}, bf16[1076,1152]{1,0:T(8,128)(2,1)}, u32[]{:S(2)}, u32[]{:S(2)}) %collective-permute-start.20) | collective-permute-done | bytes 2479136 | tf_op jit(solution)/shard_map/ppermute | solution.py:389
  305.7 36.2 %shard_map.300 = (bf16[1024,1152]{1,0:T(8,128)(2,1)}, f32[1,1152]{1,0:T(1,128)}, f32[1,1152]{1,0:T(1,128)}, f32[1,1152]{1,0:T(1,128)}, bf16[256,1152]{1,0:T(8,12...) custom-call(bf16[1024,1076]{1,0:T(8,128)(2,1)} %get-tuple-element.94.ua_ref, ...), custom_call_target="tpu_custom_call" | custom-call | flops 15231614976 | bytes 30848000 | tf_op jit(solution)/shard_map/pallas_call | solution.py:362
  348.5 18.4 %ab.5 = (bf16[3,288,1024]{2,1,0:T(8,128)(2,1)}, f32[3,288,1152]{2,1,0:T(8,128)}, f32[3,2,8,144]{3,2,1,0:T(8,128)}) custom-call(bf16[3,288,1024]{2,1,0:T(8,128)(2,1)} %get-tuple-element.106.qkv_ref, bf16[288,1024]{1,0:T(8,128)(2,1)} %fusion.34.g_ref, f32[2,8,1024]{2,1,0:T(8,128)} %get-tuple-element.107.l_ref, bf16[1024,1152]{1,0:T(8,128)(2,1)} %fusion.10.h_ref), custom_call_target="tpu_custom_call" | custom-call | flops 14118027264 | bytes 8847360 | tf_op jit(solution)/shard_map/ab/pallas_call | solution.py:140
  371.9 18.6 %ab.7 = (bf16[3,288,1024]{2,1,0:T(8,128)(2,1)}, f32[3,288,1152]{2,1,0:T(8,128)}, f32[3,2,8,144]{3,2,1,0:T(8,128)}) custom-call(bf16[3,288,1024]{2,1,0:T(8,128)(2,1)} %get-tuple-element.112.qkv_ref, bf16[288,1024]{1,0:T(8,128)(2,1)} %convolution_convert_fusion.g_ref, f32[2,8,1024]{2,1,0:T(8,128)} %get-tuple-element.113.l_ref, bf16[1024,1152]{1,0:T(8,128)(2,1)} %fusion.10.h_ref), custom_call_target="tpu_custom_call" | custom-call | flops 14118027264 | bytes 8847360 | tf_op jit(solution)/shard_map/ab/pallas_call | solution.py:140
  391.2 18.3 %ab.4 = (bf16[3,288,1024]{2,1,0:T(8,128)(2,1)}, f32[3,288,1152]{2,1,0:T(8,128)}, f32[3,2,8,144]{3,2,1,0:T(8,128)}) custom-call(bf16[3,288,1024]{2,1,0:T(8,128)(2,1)} %get-tuple-element.102.qkv_ref, bf16[288,1024]{1,0:T(8,128)(2,1)} %fusion.33.g_ref, f32[2,8,1024]{2,1,0:T(8,128)} %get-tuple-element.104.l_ref, bf16[1024,1152]{1,0:T(8,128)(2,1)} %fusion.10.h_ref), custom_call_target="tpu_custom_call" | custom-call | flops 14118027264 | bytes 8847360 | tf_op jit(solution)/shard_map/ab/pallas_call | solution.py:140
  413.1 18.3 %ab.6 = (bf16[3,288,1024]{2,1,0:T(8,128)(2,1)}, f32[3,288,1152]{2,1,0:T(8,128)}, f32[3,2,8,144]{3,2,1,0:T(8,128)}) custom-call(bf16[3,288,1024]{2,1,0:T(8,128)(2,1)} %get-tuple-element.109.qkv_ref, bf16[288,1024]{1,0:T(8,128)(2,1)} %convolution_convert_fusion.1.g_ref, f32[2,8,1024]{2,1,0:T(8,128)} %get-tuple-element.110.l_ref, bf16[1024,1152]{1,0:T(8,128)(2,1)} %fusion.10.h_ref), custom_call_target="tpu_custom_call" | custom-call | flops 14118027264 | bytes 8847360 | tf_op jit(solution)/shard_map/ab/pallas_call | solution.py:140
  431.5 22.0 %nob.1 = (bf16[256,1152]{1,0:T(8,128)(2,1)}, bf16[256,1152]{1,0:T(8,128)(2,1)}, bf16[256,1152]{1,0:T(8,128)(2,1)}, bf16[256,1152]{1,0:T(8,128)(2,1)}, f32[1,1152]{1,0:T(1,128)}, /*index=5*/f32[1,1152]{1,0:T(1,128)}) custom-call(bf16[864,1024]{1,0:T(8,128)(2,1)} %bitcast.129, bf16[864,1024]{1,0:T(8,128)(2,1)} %bitcast.127, bf16[864,1024]{1,0:T(8,128)(2,1)} %bitcast.130, ...), custom_call_target="tpu_custom_call" | custom-call | flops 8153726976 | bytes 26542080 | tf_op jit(solution)/shard_map/nob/pallas_call | solution.py:240
  466.1 7.2 %convolution_add_fusion.3 = f32[1076,1152]{1,0:T(8,128)} fusion(f32[1076,1152]{1,0:T(8,128)S(1)} %fusion.48, bf16[1024,1076]{1,0:T(8,128)(2,1)S(1)} %copy-done.49, bf16[1024,1152]{1,0:T(8,128)(2,1)} %fusion.14.h_ref), kind=kOutput, calls=%fused_computation.3 | convolution fusion | flops 2539842048 | bytes 14479360 | tf_op jit(solution)/shard_map/dot_general | solution.py:45
  479.6 10.6 %collective-permute-done.24.d_ref = bf16[256,1152]{1,0:T(8,128)(2,1)S(1)} collective-permute-done((bf16[256,1152]{1,0:T(8,128)(2,1)S(1)}, bf16[256,1152]{1,0:T(8,128)(2,1)S(1)}, u32[]{:S(2)}, u32[]{:S(2)}) %collective-permute-start.24) | collective-permute-done | bytes 589856 | tf_op jit(solution)/shard_map/ppermute | solution.py:389
  495.7 20.7 %collective-permute-done.26.c_ref = bf16[256,1152]{1,0:T(8,128)(2,1)S(1)} collective-permute-done((bf16[256,1152]{1,0:T(8,128)(2,1)S(1)}, bf16[256,1152]{1,0:T(8,128)(2,1)S(1)}, u32[]{:S(2)}, u32[]{:S(2)}) %collective-permute-start.26) | collective-permute-done | bytes 589856 | tf_op jit(solution)/shard_map/ppermute | solution.py:389
  531.8 23.4 %mof.1 = (bf16[2048,1076]{1,0:T(8,128)(2,1)}, bf16[2048,1076]{1,0:T(8,128)(2,1)}, bf16[2048,1152]{1,0:T(8,128)(2,1)}, bf16[2048,1152]{1,0:T(8,128)(2,1)}, f32[1,1076]{1,0:T(1,128)}) custom-call(s32[1]{0:T(128)} %bitcast.22.core_ref, bf16[1024,1152]{1,0:T(8,128)(2,1)} %collective-permute-done.39.ha_ref, bf16[1024,1152]{1,0:T(8,128)(2,1)} %collective-permute-done.40.hb_ref, ...), custom_call_target="tpu_custom_call" | custom-call | flops 10154409984 | bytes 18874368 | tf_op jit(solution)/shard_map/mof/pallas_call | solution.py:314
  562.0 13.1 %fusion.1 = bf16[1076,1152]{1,0:T(8,128)(2,1)} fusion(f32[1076,1152]{1,0:T(8,128)} %convolution_add_fusion.2, bf16[2048,1076]{1,0:T(8,128)(2,1)} %get-tuple-element.145, bf16[2048,1152]{1,0:T(8,128)(2,1)} %get-tuple-element.146), kind=kOutput, calls=%fused_computation.5 | convolution fusion | flops 5079684096 | bytes 16563200 | tf_op jit(solution)/shard_map/dot_general | solution.py:45
  575.2 7.8 %fusion.2 = bf16[1152,1076]{0,1:T(8,128)(2,1)} fusion(f32[1076,1152]{1,0:T(8,128)S(1)} %bitcast.133, bf16[2048,1076]{1,0:T(8,128)(2,1)S(1)} %bitcast.135, bf16[2048,1152]{1,0:T(8,128)(2,1)S(1)} %bitcast.137), kind=kOutput, calls=%fused_computation.9 | convolution fusion | flops 5079684096 | bytes 16563200 | tf_op jit(solution)/shard_map/dot_general | solution.py:45
  586.7 61.5 %collective-permute-done.32 = f32[3,288,1152]{2,1,0:T(8,128)S(1)} collective-permute-done((f32[3,288,1152]{2,1,0:T(8,128)S(1)}, f32[3,288,1152]{2,1,0:T(8,128)S(1)}, u32[]{:S(2)}, u32[]{:S(2)}) %collective-permute-start.32) | collective-permute-done | bytes 3981344 | tf_op jit(solution)/shard_map/ppermute | solution.py:389
  (282 shorter events, 155.8 us)
Async XLA Ops:
  10.0 93.8 %collective-permute-start.5 = (bf16[3,288,1152]{2,1,0:T(8,128)(2,1)}, bf16[3,288,1152]{2,1,0:T(8,128)(2,1)}, u32[]{:S(2)}, u32[]{:S(2)}) collective-permute-start(bf16[3,288,1152]{2,1,0:T(8,128)(2,1)} %pad_maximum_fusion.1.w_ref), channel_id=1, source_target_pairs={{0,2},{1,3},{2,0},{3,1},{4,6},{5,7},{6,4},{7,5},{8,10},{9,11},{10,... | collective-permute-start | bytes 5971976 | tf_op jit(solution)/shard_map/ppermute | solution.py:389
  11.7 56.4 %collective-permute-start.2 = (bf16[256,1152]{1,0:T(8,128)(2,1)}, bf16[256,1152]{1,0:T(8,128)(2,1)S(1)}, u32[]{:S(2)}, u32[]{:S(2)}) collective-permute-start(bf16[256,1152]{1,0:T(8,128)(2,1)} %get-tuple-element.161), channel_id=1, source_target_pairs={{0,3},{1,2},{2,1},{3,0},{4,7},{5,6},{6,5},{7,4},{8,11},{9,10},{10,... | collective-permute-start | bytes 1769480 | tf_op jit(solution)/shard_map/ppermute | solution.py:389
  14.9 66.3 %collective-permute-start.1 = (bf16[256,1152]{1,0:T(8,128)(2,1)S(1)}, bf16[256,1152]{1,0:T(8,128)(2,1)S(1)}, u32[]{:S(2)}, u32[]{:S(2)}) collective-permute-start(bf16[256,1152]{1,0:T(8,128)(2,1)S(1)} %get-tuple-element.162), channel_id=1, source_target_pairs={{0,2},{1,3},{2,0},{3,1},{4,6},{5,7},{6,4},{7,5},{8,10},{9,11},{10,... | collective-permute-start | bytes 1769480 | tf_op jit(solution)/shard_map/ppermute | solution.py:389
  16.3 75.2 %collective-permute-start.3 = (bf16[3,288,1152]{2,1,0:T(8,128)(2,1)}, bf16[3,288,1152]{2,1,0:T(8,128)(2,1)}, u32[]{:S(2)}, u32[]{:S(2)}) collective-permute-start(bf16[3,288,1152]{2,1,0:T(8,128)(2,1)} %pad_maximum_fusion.1.w_ref), channel_id=1, source_target_pairs={{0,1},{1,0},{2,3},{3,2},{4,5},{5,4},{6,7},{7,6},{8,9},{9,8},{10,11... | collective-permute-start | bytes 5971976 | tf_op jit(solution)/shard_map/ppermute | solution.py:389
  103.8 37.4 %collective-permute-start.7 = (bf16[3,288,1152]{2,1,0:T(8,128)(2,1)}, bf16[3,288,1152]{2,1,0:T(8,128)(2,1)}, u32[]{:S(2)}, u32[]{:S(2)}) collective-permute-start(bf16[3,288,1152]{2,1,0:T(8,128)(2,1)} %collective-permute-done.5.w_ref), channel_id=1, source_target_pairs={{0,1},{1,0},{2,3},{3,2},{4,5},{5,4},{6,7},{7,6},{8,9},{9,8},{10,11... | collective-permute-start | bytes 5971976 | tf_op jit(solution)/shard_map/ppermute | solution.py:389
  104.2 49.7 %collective-permute-start.9 = (bf16[288,1152]{1,0:T(8,128)(2,1)}, bf16[288,1152]{1,0:T(8,128)(2,1)}, u32[]{:S(2)}, u32[]{:S(2)}) collective-permute-start(bf16[288,1152]{1,0:T(8,128)(2,1)} %bitcast.19), channel_id=1, source_target_pairs={{0,1},{1,0},{2,3},{3,2},{4,5},{5,4},{6,7},{7,6},{8,9},{9,8},{10,11... | collective-permute-start | bytes 1990664 | tf_op jit(solution)/shard_map/ppermute | solution.py:389
  107.2 67.9 %collective-permute-start.15 = (bf16[2,256,1152]{2,1,0:T(8,128)(2,1)}, bf16[2,256,1152]{2,1,0:T(8,128)(2,1)}, u32[]{:S(2)}, u32[]{:S(2)}) collective-permute-start(bf16[2,256,1152]{2,1,0:T(8,128)(2,1)} %get-tuple-element.157.dc_ref), channel_id=1, source_target_pairs={{0,2},{1,3},{2,0},{3,1},{4,6},{5,7},{6,4},{7,5},{8,10},{9,11},{10,... | collective-permute-start | bytes 3538952 | tf_op jit(solution)/shard_map/ppermute | solution.py:389
  109.0 67.0 %collective-permute-start.14 = (bf16[2,256,1152]{2,1,0:T(8,128)(2,1)S(1)}, bf16[2,256,1152]{2,1,0:T(8,128)(2,1)}, u32[]{:S(2)}, u32[]{:S(2)}) collective-permute-start(bf16[2,256,1152]{2,1,0:T(8,128)(2,1)S(1)} %get-tuple-element.158.b_ref.a_ref), channel_id=1, source_target_pairs={{0,1},{1,0},{2,3},{3,2},{4,5},{5,4},{6,7},{7,6},{8,9},{9,8},{10,11... | collective-permute-start | bytes 3538952 | tf_op jit(solution)/shard_map/ppermute | solution.py:389
  175.2 42.3 %collective-permute-start.13 = (bf16[1024,1152]{1,0:T(8,128)(2,1)}, bf16[1024,1152]{1,0:T(8,128)(2,1)}, u32[]{:S(2)}, u32[]{:S(2)}) collective-permute-start(bf16[1024,1152]{1,0:T(8,128)(2,1)} %fusion.14.h_ref), channel_id=1, source_target_pairs={{0,1},{1,0},{2,3},{3,2},{4,5},{5,4},{6,7},{7,6},{8,9},{9,8},{10,11... | collective-permute-start | bytes 7077896 | tf_op jit(solution)/shard_map/ppermute | solution.py:389
  175.7 56.3 %collective-permute-start.12 = (bf16[1076,1152]{1,0:T(8,128)(2,1)}, bf16[1076,1152]{1,0:T(8,128)(2,1)}, u32[]{:S(2)}, u32[]{:S(2)}) collective-permute-start(bf16[1076,1152]{1,0:T(8,128)(2,1)} %bitcast.123), channel_id=1, source_target_pairs={{0,2},{1,3},{2,0},{3,1},{4,6},{5,7},{6,4},{7,5},{8,10},{9,11},{10,... | collective-permute-start | bytes 7437320 | tf_op jit(solution)/shard_map/ppermute | solution.py:389
  232.0 56.7 %collective-permute-start.20 = (bf16[1076,1152]{1,0:T(8,128)(2,1)}, bf16[1076,1152]{1,0:T(8,128)(2,1)}, u32[]{:S(2)}, u32[]{:S(2)}) collective-permute-start(bf16[1076,1152]{1,0:T(8,128)(2,1)} %w2_ref.3), channel_id=1, source_target_pairs={{0,2},{1,3},{2,0},{3,1},{4,6},{5,7},{6,4},{7,5},{8,10},{9,11},{10,... | collective-permute-start | bytes 7437320 | tf_op jit(solution)/shard_map/ppermute | solution.py:389
  288.7 174.7 %collective-permute-start.41 = (bf16[2,256,1152]{2,1,0:T(8,128)(2,1)S(1)}, bf16[2,256,1152]{2,1,0:T(8,128)(2,1)}, u32[]{:S(2)}, u32[]{:S(2)}) collective-permute-start(bf16[2,256,1152]{2,1,0:T(8,128)(2,1)S(1)} %copy-done.2), channel_id=1, source_target_pairs={{0,2},{1,3},{2,0},{3,1},{4,6},{5,7},{6,4},{7,5},{8,10},{9,11},{10,... | collective-permute-start | bytes 3538952 | tf_op jit(solution)/shard_map/ppermute | solution.py:389
  295.3 160.8 %collective-permute-start.39 = (bf16[1024,1152]{1,0:T(8,128)(2,1)}, bf16[1024,1152]{1,0:T(8,128)(2,1)}, u32[]{:S(2)}, u32[]{:S(2)}) collective-permute-start(bf16[1024,1152]{1,0:T(8,128)(2,1)} %fusion.14.h_ref), channel_id=1, source_target_pairs={{0,2},{1,3},{2,0},{3,1},{4,6},{5,7},{6,4},{7,5},{8,10},{9,11},{10,... | collective-permute-start | bytes 7077896 | tf_op jit(solution)/shard_map/ppermute | solution.py:389
  345.6 120.0 %collective-permute-start.22 = (bf16[256,1152]{1,0:T(8,128)(2,1)}, bf16[256,1152]{1,0:T(8,128)(2,1)S(1)}, u32[]{:S(2)}, u32[]{:S(2)}) collective-permute-start(bf16[256,1152]{1,0:T(8,128)(2,1)} %get-tuple-element.99), channel_id=1, source_target_pairs={{0,1},{1,0},{2,3},{3,2},{4,5},{5,4},{6,7},{7,6},{8,9},{9,8},{10,11... | collective-permute-start | bytes 1769480 | tf_op jit(solution)/shard_map/ppermute | solution.py:389
  367.7 96.2 %collective-permute-start.33 = (f32[3,2,144]{2,1,0:T(2,128)S(1)}, f32[3,2,144]{2,1,0:T(2,128)S(1)}, u32[]{:S(2)}, u32[]{:S(2)}) collective-permute-start(f32[3,2,144]{2,1,0:T(2,128)S(1)} %slice_bitcast_fusion.1), channel_id=1, source_target_pairs={{0,1},{1,0},{2,3},{3,2},{4,5},{5,4},{6,7},{7,6},{8,9},{9,8},{10,11... | collective-permute-start | bytes 10376 | tf_op jit(solution)/shard_map/ppermute | solution.py:389
  391.2 63.1 %collective-permute-start.34 = (f32[3,2,144]{2,1,0:T(2,128)S(1)}, f32[3,2,144]{2,1,0:T(2,128)S(1)}, u32[]{:S(2)}, u32[]{:S(2)}) collective-permute-start(f32[3,2,144]{2,1,0:T(2,128)S(1)} %bitcast.120), channel_id=1, source_target_pairs={{0,1},{1,0},{2,3},{3,2},{4,5},{5,4},{6,7},{7,6},{8,9},{9,8},{10,11... | collective-permute-start | bytes 10376 | tf_op jit(solution)/shard_map/ppermute | solution.py:389
  465.6 66.2 %collective-permute-start.40 = (bf16[1024,1152]{1,0:T(8,128)(2,1)}, bf16[1024,1152]{1,0:T(8,128)(2,1)}, u32[]{:S(2)}, u32[]{:S(2)}) collective-permute-start(bf16[1024,1152]{1,0:T(8,128)(2,1)} %collective-permute-done.39.ha_ref), channel_id=1, source_target_pairs={{0,1},{1,0},{2,3},{3,2},{4,5},{5,4},{6,7},{7,6},{8,9},{9,8},{10,11... | collective-permute-start | bytes 7077896 | tf_op jit(solution)/shard_map/ppermute | solution.py:389
  465.6 90.9 %collective-permute-start.31 = (f32[3,288,1152]{2,1,0:T(8,128)}, f32[3,288,1152]{2,1,0:T(8,128)}, u32[]{:S(2)}, u32[]{:S(2)}) collective-permute-start(f32[3,288,1152]{2,1,0:T(8,128)} %get-tuple-element.128), channel_id=1, source_target_pairs={{0,1},{1,0},{2,3},{3,2},{4,5},{5,4},{6,7},{7,6},{8,9},{9,8},{10,11... | collective-permute-start | bytes 11943944 | tf_op jit(solution)/shard_map/ppermute | solution.py:389
  479.6 36.7 %collective-permute-start.27 = (bf16[256,1152]{1,0:T(8,128)(2,1)S(1)}, bf16[256,1152]{1,0:T(8,128)(2,1)S(1)}, u32[]{:S(2)}, u32[]{:S(2)}) collective-permute-start(bf16[256,1152]{1,0:T(8,128)(2,1)S(1)} %copy-done.39), channel_id=1, source_target_pairs={{0,3},{1,2},{2,1},{3,0},{4,7},{5,6},{6,5},{7,4},{8,11},{9,10},{10,... | collective-permute-start | bytes 1769480 | tf_op jit(solution)/shard_map/ppermute | solution.py:389
  493.9 32.7 %collective-permute-start.37 = (f32[288,1152]{1,0:T(8,128)}, f32[288,1152]{1,0:T(8,128)}, u32[]{:S(2)}, u32[]{:S(2)}) collective-permute-start(f32[288,1152]{1,0:T(8,128)} %fusion.47), channel_id=1, source_target_pairs={{0,1},{1,0},{2,3},{3,2},{4,5},{5,4},{6,7},{7,6},{8,9},{9,8},{10,11... | collective-permute-start | bytes 3981320 | tf_op jit(solution)/shard_map/ppermute | solution.py:389
  526.6 56.3 %collective-permute-start.36 = (f32[288,1152]{1,0:T(8,128)S(1)}, f32[288,1152]{1,0:T(8,128)}, u32[]{:S(2)}, u32[]{:S(2)}) collective-permute-start(f32[288,1152]{1,0:T(8,128)S(1)} %fusion.46), channel_id=1, source_target_pairs={{0,1},{1,0},{2,3},{3,2},{4,5},{5,4},{6,7},{7,6},{8,9},{9,8},{10,11... | collective-permute-start | bytes 3981320 | tf_op jit(solution)/shard_map/ppermute | solution.py:389
  530.9 55.8 %collective-permute-start.30 = (f32[3,288,1152]{2,1,0:T(8,128)}, f32[3,288,1152]{2,1,0:T(8,128)}, u32[]{:S(2)}, u32[]{:S(2)}) collective-permute-start(f32[3,288,1152]{2,1,0:T(8,128)} %get-tuple-element.126), channel_id=1, source_target_pairs={{0,1},{1,0},{2,3},{3,2},{4,5},{5,4},{6,7},{7,6},{8,9},{9,8},{10,11... | collective-permute-start | bytes 11943944 | tf_op jit(solution)/shard_map/ppermute | solution.py:389
  531.3 51.6 %collective-permute-start.38 = (f32[288,1152]{1,0:T(8,128)}, f32[288,1152]{1,0:T(8,128)}, u32[]{:S(2)}, u32[]{:S(2)}) collective-permute-start(f32[288,1152]{1,0:T(8,128)} %convolution_add_fusion.4), channel_id=1, source_target_pairs={{0,2},{1,3},{2,0},{3,1},{4,6},{5,7},{6,4},{7,5},{8,10},{9,11},{10,... | collective-permute-start | bytes 3981320 | tf_op jit(solution)/shard_map/ppermute | solution.py:389
  560.4 87.8 %collective-permute-start.32 = (f32[3,288,1152]{2,1,0:T(8,128)S(1)}, f32[3,288,1152]{2,1,0:T(8,128)S(1)}, u32[]{:S(2)}, u32[]{:S(2)}) collective-permute-start(f32[3,288,1152]{2,1,0:T(8,128)S(1)} %add.132), channel_id=1, source_target_pairs={{0,2},{1,3},{2,0},{3,1},{4,6},{5,7},{6,4},{7,5},{8,10},{9,11},{10,... | collective-permute-start | bytes 11943944 | tf_op jit(solution)/shard_map/ppermute | solution.py:389
  (78 other events, 1394.8 us)
